TPU v7x, 32 devices: a whole 2x2x4 slice. The times are simulated.
32 devices in a mesh: graph: 8 (over z, x), mp: 4 (over y, core).
Axes of the slice: x: 2, y: 2, z: 4, core: 2. Of those that a mesh axis runs over, the one named last changes fastest.
Arguments:
- edge_state: bfloat16 [4096, 1536], P('graph', 'mp'), may hold values from -6 to 6
- down_weight: bfloat16 [1536, 384], P('mp'), may hold values from -0.15625 to 0.15625
- basis: float32 [42, 131072], P(None, ('graph', 'mp')), may hold values from -6 to 6
- basis_weight: float32 [42, 384], replicated, may hold values from -1 to 1
- up_weight: bfloat16 [384, 1536], P(None, 'mp'), may hold values from -0.3125 to 0.3125
- dense_weight: bfloat16 [3, 2, 1536, 1536], P(None, None, None, 'mp'), may hold values from -0.15625 to 0.15625
- send_rows: int32 [8, 32, 64], P('graph', 'mp'), may hold values from 0 to 512, as said below
- trip_in: int32 [131072], P(('graph', 'mp')), may hold values from 0 to 511, as said below
- trip_out: int32 [131072], P(('graph', 'mp')), may hold values from 0 to 511, as said below
- trip_live: int32 [131072], P(('graph', 'mp')), may hold values from 0 to 1, as said below
- edge_atom: int32 [4096], P('graph'), may hold values from 0 to 255
Outputs:
- edge_out: bfloat16 [4096, 1536], P('graph', 'mp')
- atom_out: bfloat16 [256, 1536], P('graph', 'mp')
Inputs may be any that keep to these rules, and one draw needn't show every extreme that they name: `send_rows`: entry [s, m * 8 + g, c] is a row among the 512 edges of graph index s listed in slot c for the device at graph index g and mp index m, or 512 for an empty slot; used slots come first in each list, and some device has every list full. `trip_in`: A slot s * 64 + c of the triplet's own device whose list entry from graph index s is used. `trip_out`: A slot s * 64 + c of the triplet's own device whose list entry from graph index s is used. `trip_live`: on each device the real triplets come first; some device has no padding.
All inputs are finite; a program needn't handle non-finite values.
Results may differ from a plain program's by a relative error of at most 0.014.
Values may be sent and summed in bfloat16 or wider, within the bound.
A program may use at most 128 MiB of HBM per device.

v0:
```python
import functools

import jax
import jax.numpy as jnp
from jax import lax
from jax.experimental import pallas as pl
from jax.experimental.pallas import tpu as pltpu
from jax.sharding import PartitionSpec as P

ATOM_DEV = 32
CHUNKS = 4

inv_root_two = 0.7071067811865476
atom_scale = 0.2

MESH = pl.DeviceIdType.MESH
bf16 = jnp.bfloat16
f32 = jnp.float32


def silu(v):
    return v / (1.0 + jnp.exp(-v))


def flip(index, bit):
    return index + bit - 2 * bit * ((index // bit) % 2)


def one_hot(rows, ids):
    shape = (rows, ids.shape[1])
    return jnp.where(lax.broadcasted_iota(jnp.int32, shape, 0) == ids, 1.0, 0.0).astype(bf16)


def dot(a, b, ca=1, cb=0):
    return lax.dot_general(a, b, (((ca,), (cb,)), ((), ())), preferred_element_type=f32)


def gather_plan(mp):
    plan, held, bit = [], [0], mp // 2
    while bit >= 1:
        plan += [(bit, off) for off in held]
        held += [bit ^ off for off in held]
        bit //= 2
    return plan, held


def kernel(
    graph, mp, tile,
    state_ref, down_ref, basis_ref, bw_ref, up_ref, dense_hbm, lists_ref, in_ref, out_ref, live_ref, atom_ref,
    edge_out_ref, atom_out_ref,
    weight, weight_sem,
    part_a, got_a, sum_a, more_a, full_a,
    part_b, got_b, sum_b, more_b, full_b,
    red_send, red_recv,
    to_a, from_a, to_b, from_b, xc_send, xc_recv,
    lists_flat, list_hot, angle, slots, in_hot, out_hot,
    acts, hidden, act_send, act_recv,
    atoms_own, atoms_to, atoms_from, table,
):
    g = lax.axis_index("graph")
    m = lax.axis_index("mp")
    rows, width = state_ref.shape
    trip = down_ref.shape[1]
    layers = weight.shape[0] // 2
    cap = lists_ref.shape[2]
    slot_total = graph * cap
    pieces, lane = to_a.shape[0], to_a.shape[2]
    kept = in_hot is not None
    triplets = in_ref.shape[1]
    atoms = graph * ATOM_DEV
    half = rows // 2
    bits = [1 << i for i in range(mp.bit_length() - 1)]

    load = pltpu.make_async_copy(dense_hbm, weight, weight_sem)
    load.start()

    barrier = pltpu.get_barrier_semaphore()

    def greet(k, _):
        pl.semaphore_signal(barrier, inc=1, device_id={"graph": (g + k) % graph}, device_id_type=MESH)
        return 0

    lax.fori_loop(1, graph, greet, 0)
    for bit in bits:
        pl.semaphore_signal(barrier, inc=1, device_id={"mp": flip(m, bit)}, device_id_type=MESH)

    def mp_copy(src, dst, which, slot, i, bit):
        return pltpu.make_async_remote_copy(
            src_ref=src, dst_ref=dst, send_sem=red_send.at[which, slot, i], recv_sem=red_recv.at[which, slot, i],
            device_id={"mp": flip(m, bit)}, device_id_type=MESH)

    mine = pl.multiple_of((m % 2) * half, half)
    other = pl.multiple_of(half - (m % 2) * half, half)
    size = rows // CHUNKS
    subs = range(CHUNKS // 2)

    def mp_sum(which, part, got, summed, more, full, meanwhile=None, ready=None):
        at = [pl.ds(i * size, size) for i in subs]
        firsts = [mp_copy(part.at[pl.ds(other + i * size, size)], got.at[at[i]], which, 0, i, 1) for i in subs]
        steps = [[mp_copy(summed.at[b, at[i]], more.at[b, at[i]], which, 1 + b, i, bit) for i in subs]
                 for b, bit in enumerate(bits[1:])]
        for first in firsts:
            first.start()

        def total(b, i):
            if b == 0:
                return part[pl.ds(mine + i * size, size)].astype(f32) + got[at[i]].astype(f32)
            return summed[b - 1, at[i]].astype(f32) + more[b - 1, at[i]].astype(f32)

        for b in range(len(bits) - 1):
            for i in subs:
                (firsts[i] if b == 0 else steps[b - 1][i]).wait()
                summed[b, at[i]] = total(b, i).astype(bf16)
                steps[b][i].start()
        if meanwhile is not None:
            meanwhile()
        lasts = []
        for i in subs:
            (firsts[i] if len(bits) == 1 else steps[-1][i]).wait()
            here = pl.ds(mine + i * size, size)
            full[here] = total(len(bits) - 1, i).astype(bf16)
            lasts.append(mp_copy(full.at[here], full.at[here], which, len(bits), i, 1))
            lasts[i].start()
            if ready is not None:
                lasts[i].wait()
                ready(i)
        if ready is None:
            for last in lasts:
                last.wait()

    def exchange(which, src_at, dst, dst_at, size):
        def copy(k):
            peer = (g + k) % graph
            return pltpu.make_async_remote_copy(
                src_ref=src_at(peer), dst_ref=dst_at(g),
                send_sem=xc_send.at[which, k], recv_sem=xc_recv.at[which, k],
                device_id={"graph": peer}, device_id_type=MESH)

        def start(k, _):
            copy(k).start()
            return 0

        def wait(k, _):
            copy(k).wait()
            return 0

        return (lambda: lax.fori_loop(1, graph, start, 0)), (lambda: lax.fori_loop(1, graph, wait, 0))

    def block(ref, size):
        return lambda i: ref.at[pl.ds(pl.multiple_of(i * size, size), size)]

    def piece(ref, j, size):
        return lambda i: ref.at[j, pl.ds(pl.multiple_of(i * size, size), size)]

    def tiles(step):
        def one(i, _):
            step(pl.ds(pl.multiple_of(i * tile, tile), tile))
            return 0

        lax.fori_loop(0, triplets // tile, one, 0)

    def in_part(at):
        return one_hot(slot_total, in_ref[:, at])

    def out_part(at):
        return one_hot(slot_total, jnp.where(live_ref[:, at] > 0, out_ref[:, at], -1))

    def angles(at):
        angle[:, at] = lax.dot_general(
            bw_ref[...], basis_ref[:, at], (((0,), (0,)), ((), ())),
            precision=lax.Precision.HIGHEST, preferred_element_type=f32)

    part_a[...] = dot(state_ref[...], down_ref[...]).astype(bf16)
    for i in range(graph):
        lists_flat[:, i * cap:(i + 1) * cap] = lists_ref[0, i:i + 1, :]
    list_hot[...] = one_hot(rows, lists_flat[...])
    pl.semaphore_wait(barrier, graph - 1 + len(bits))
    mp_sum(0, part_a, got_a, sum_a, more_a, full_a, lambda: tiles(angles))

    step_rows = min(slot_total, 512)
    own = pl.ds(pl.multiple_of(g * cap, cap), cap)

    def pick(i, _):
        at = pl.ds(pl.multiple_of(i * step_rows, step_rows), step_rows)
        picked = dot(list_hot[:, at], full_a[...], 0, 0).astype(bf16)
        for j in range(pieces):
            to_a[j, at, :] = picked[:, j * lane:(j + 1) * lane]
        return 0

    lax.fori_loop(0, slot_total // step_rows, pick, 0)
    going = [exchange(j, piece(to_a, j, cap), from_a, piece(from_a, j, cap), cap) for j in range(pieces)]
    back = [exchange(pieces + j, piece(to_b, j, cap), from_b, piece(from_b, j, cap), cap) for j in range(pieces)]
    for start, _ in going:
        start()
    for j in range(pieces):
        from_a[j, own] = to_a[j, own]
    if kept:
        def keep(at):
            in_hot[:, at] = in_part(at)
            out_hot[:, at] = out_part(at)

        tiles(keep)

    for j in range(pieces):
        going[j][1]()
        slots[...] = jnp.zeros_like(slots)
        received = from_a[j].astype(f32).T.astype(bf16)

        def trips(at):
            source = in_hot[:, at] if kept else in_part(at)
            value = dot(received, source) * angle[j * lane:(j + 1) * lane, at]
            target = out_hot[:, at] if kept else out_part(at)
            slots[...] += dot(target, value.astype(bf16), 1, 1)

        tiles(trips)
        to_b[j] = slots[...].astype(bf16)
        back[j][0]()
        from_b[j, own] = to_b[j, own]

    for j in range(pieces):
        back[j][1]()
        part_b[:, j * lane:(j + 1) * lane] = dot(list_hot[...], from_b[j]).astype(bf16)

    plan, held = gather_plan(mp)
    order = [h * len(subs) + i for i in subs for h in (0, 1)]

    def other_of(off):
        index = m
        for bit in bits:
            if off & bit:
                index = flip(index, bit)
        return index

    def act_copy(layer, c, which):
        bit, off = plan[which]
        at = acts.at[layer, other_of(off), pl.ds(c * size, size)]
        return pltpu.make_async_remote_copy(
            src_ref=at, dst_ref=at,
            send_sem=act_send.at[layer, c, which], recv_sem=act_recv.at[layer, c, which],
            device_id={"mp": flip(m, bit)}, device_id_type=MESH)

    local = [i for i, (bit, off) in enumerate(plan) if off == 0]
    relayed = [i for i, (bit, off) in enumerate(plan) if off != 0]
    brings = {bit ^ off: i for i, (bit, off) in enumerate(plan)}
    relays_from = sorted({brings[plan[i][1]] for i in relayed})

    def send(layer, c):
        for i in local:
            act_copy(layer, c, i).start()

    def relay(layer, c):
        for i in relayed:
            first = brings[plan[i][1]]
            if [j for j in relayed if brings[plan[j][1]] == first][0] == i:
                act_copy(layer, c, first).wait_recv()
            act_copy(layer, c, i).start()

    def finish(layer, c):
        for i in range(len(plan)):
            if i not in relays_from:
                act_copy(layer, c, i).wait_recv()

    def begin(i):
        for c in order[2 * i:2 * i + 2]:
            at = pl.ds(c * size, size)
            first = state_ref[at, :].astype(f32) + dot(full_b[at, :], up_ref[...])
            hidden[at, :] = first
            acts[0, m, at, :] = first.astype(bf16)
            send(0, c)

    mp_sum(1, part_b, got_b, sum_b, more_b, full_b, ready=begin)
    load.wait()
    relay(0, order[0])

    def layer_step(l, _):
        for inside in range(2):
            k = 2 * l + inside
            for spot, c in enumerate(order):
                at = pl.ds(c * size, size)
                if spot + 1 < CHUNKS:
                    relay(k, order[spot + 1])
                elif inside == 0:
                    relay(k + 1, order[0])
                else:
                    @pl.when(l + 1 < layers)
                    def _():
                        relay(k + 1, order[0])
                finish(k, c)
                total = None
                for off in held:
                    index = other_of(off)
                    term = dot(acts[k, index, at, :], weight[k, pl.ds(pl.multiple_of(index * width, width), width), :])
                    total = term if total is None else total + term
                value = silu(total)
                if inside == 0:
                    acts[k + 1, m, at, :] = value.astype(bf16)
                    send(k + 1, c)
                else:
                    value = (hidden[at, :] + value) * inv_root_two
                    hidden[at, :] = value

                    @pl.when(l + 1 < layers)
                    def _():
                        acts[k + 1, m, at, :] = value.astype(bf16)
                        send(k + 1, c)
        return 0

    lax.fori_loop(0, layers, layer_step, 0)

    atom_rows = min(atoms, 256)

    def collect(i, _):
        at = pl.ds(pl.multiple_of(i * atom_rows, atom_rows), atom_rows)
        ids = one_hot(atom_rows, atom_ref[...] - i * atom_rows)
        high = hidden[...].astype(bf16)
        low = (hidden[...] - high.astype(f32)).astype(bf16)
        total = dot(ids, high) + dot(ids, low)
        atoms_own[at, :] = total
        atoms_to[at, :] = total.astype(bf16)
        return 0

    lax.fori_loop(0, atoms // atom_rows, collect, 0)
    start, wait = exchange(2 * pieces, block(atoms_to, ATOM_DEV), atoms_from, block(atoms_from, ATOM_DEV), ATOM_DEV)
    start()
    here = pl.ds(pl.multiple_of(g * ATOM_DEV, ATOM_DEV), ATOM_DEV)
    atoms_from[here] = jnp.zeros((ATOM_DEV, width), bf16)
    wait()

    def add(i, total):
        return total + atoms_from[pl.ds(pl.multiple_of(i * ATOM_DEV, ATOM_DEV), ATOM_DEV)].astype(f32)

    total = lax.fori_loop(0, graph, add, atoms_own[here])
    mine_out = silu(atom_scale * total).astype(bf16)
    table[here] = mine_out
    atom_out_ref[...] = mine_out
    start, wait = exchange(2 * pieces + 1, lambda peer: block(table, ATOM_DEV)(g), table, block(table, ATOM_DEV), ATOM_DEV)
    start()

    def drain(k, _):
        for c in range(CHUNKS):
            for i in range(len(plan)):
                act_copy(k, c, i).wait_send()
        return 0

    lax.fori_loop(0, 2 * layers, drain, 0)
    wait()

    def spread(i, _):
        at = pl.ds(pl.multiple_of(i * atom_rows, atom_rows), atom_rows)
        hidden[...] += dot(one_hot(atom_rows, atom_ref[...] - i * atom_rows), table[at, :], 0, 0)
        return 0

    lax.fori_loop(0, atoms // atom_rows, spread, 0)
    edge_out_ref[...] = hidden[...].astype(bf16)


def hand_on(edge_ref, atom_ref, edge_out_ref, atom_out_ref):
    edge_out_ref[...] = edge_ref[...]
    atom_out_ref[...] = atom_ref[...]


def local(graph, mp, edge_state, down_weight, basis, basis_weight, up_weight, dense_weight,
          send_rows, trip_in, trip_out, trip_live, edge_atom):
    rows, width = edge_state.shape
    trip = down_weight.shape[1]
    slot_total = graph * send_rows.shape[2]
    triplets = trip_in.shape[0]
    maps = dense_weight.shape[0] * dense_weight.shape[1]
    tile = 2048 if slot_total <= 512 else 128
    atoms = graph * ATOM_DEV
    stages = mp.bit_length()
    extra = max(stages - 2, 1)
    half = rows // 2
    vmem = pltpu.VMEM
    pieces = trip // 128 if trip % 128 == 0 else 1
    hot_bytes = 2 * 2 * slot_total * triplets
    hots = [vmem((slot_total, triplets), bf16)] * 2 if hot_bytes <= 2 ** 24 else [None, None]
    reduce_bufs = [
        vmem((rows, trip), bf16), vmem((half, trip), bf16), vmem((extra, half, trip), bf16),
        vmem((extra, half, trip), bf16), vmem((rows, trip), bf16),
    ]
    dma = pltpu.SemaphoreType.DMA
    spec = pl.BlockSpec(memory_space=pltpu.VMEM)
    body = functools.partial(kernel, graph, mp, tile)
    if hots[0] is None:
        hots, kept_body, at = [], body, 37
        body = lambda *refs: kept_body(*refs[:at], None, None, *refs[at:])
    outs = pl.pallas_call(
        body,
        out_shape=(
            jax.ShapeDtypeStruct((rows, width), bf16),
            jax.ShapeDtypeStruct((ATOM_DEV, width), bf16),
        ),
        in_specs=[spec] * 5 + [pl.BlockSpec(memory_space=pl.ANY)] + [spec] * 5,
        out_specs=(spec, spec),
        scratch_shapes=[
            vmem((maps,) + dense_weight.shape[2:], bf16), dma(()),
            *reduce_bufs, *reduce_bufs,
            dma((2, stages, CHUNKS // 2)), dma((2, stages, CHUNKS // 2)),
            *[vmem((pieces, slot_total, trip // pieces), bf16)] * 4,
            dma((2 * pieces + 2, graph)), dma((2 * pieces + 2, graph)),
            vmem((1, slot_total), jnp.int32), vmem((rows, slot_total), bf16),
            vmem((trip, triplets), f32), vmem((slot_total, trip // pieces), f32), *hots,
            vmem((maps, mp, rows, width), bf16), vmem((rows, max(width, trip)), f32),
            dma((maps, CHUNKS, mp - 1)), dma((maps, CHUNKS, mp - 1)),
            vmem((atoms, width), f32), vmem((atoms, width), bf16), vmem((atoms, width), bf16),
            vmem((atoms, width), bf16),
        ],
        compiler_params=pltpu.CompilerParams(
            collective_id=0, has_side_effects=True, vmem_limit_bytes=64000 * 1024
        ),
        name="edge_block",
    )(
        edge_state, down_weight, basis, basis_weight, up_weight,
        dense_weight.reshape((maps,) + dense_weight.shape[2:]),
        send_rows, trip_in.reshape(1, triplets), trip_out.reshape(1, triplets),
        trip_live.reshape(1, triplets), edge_atom.reshape(1, rows),
    )
    return pl.pallas_call(
        hand_on,
        out_shape=tuple(jax.ShapeDtypeStruct(o.shape, o.dtype) for o in outs),
        in_specs=[spec] * 2,
        out_specs=(spec, spec),
        name="hand_on",
    )(*outs)


def solution(mesh):
    in_specs = (
        P("graph", "mp"),
        P("mp", None),
        P(None, ("graph", "mp")),
        P(),
        P(None, "mp"),
        P(None, None, None, "mp"),
        P("graph", "mp", None),
        P(("graph", "mp")),
        P(("graph", "mp")),
        P(("graph", "mp")),
        P("graph"),
    )
    out_specs = (P("graph", "mp"), P("graph", "mp"))
    body = functools.partial(local, mesh.shape["graph"], mesh.shape["mp"])
    return jax.shard_map(body, mesh=mesh, in_specs=in_specs, out_specs=out_specs, check_vma=False)
```

profile of v0, /device:TPU:0, one launch (start us, length us, event | category | flops | bytes accessed | tf_op | source)
XLA Modules:
  0.0 116.1 jit_solution(4743877682821652171)
XLA Ops:
  0.6 113.7 %edge_block.1 = (bf16[512,384]{1,0:T(8,128)(2,1)}, bf16[32,384]{1,0:T(8,128)(2,1)}) custom-call(bf16[512,384]{1,0:T(8,128)(2,1)} %state_ref.1, bf16[384,384]{1,0:T(8,128)(2,1)} %down_ref.1, f32[42,4096]{1,0:T(8,128)} %basis_ref.1, f32[42,384]{1,0:T(8,128)} %bw_ref.1, bf16[384,384]{1,0:T(8,128)(2,1)} %up_ref.1, bf16[6,1536,384]{2,1,0:T(8,128)(2,1)} %bitcast.5, ...), custom_call_target="tpu_custom_call" | custom-call | tf_op jit(solution)/shard_map/edge_block/pallas_call | solution.py:388
  114.3 1.8 %hand_on.1 = (bf16[512,384]{1,0:T(8,128)(2,1)}, bf16[32,384]{1,0:T(8,128)(2,1)}) custom-call(bf16[512,384]{1,0:T(8,128)(2,1)} %get-tuple-element.4.edge_ref, bf16[32,384]{1,0:T(8,128)(2,1)} %get-tuple-element.5.atom_ref), custom_call_target="tpu_custom_call" | custom-call | tf_op jit(solution)/shard_map/hand_on/pallas_call | solution.py:419
where the time goes:
time: 116 us
  Pallas kernels  115 us (99%)
    pallas_call x1, Pallas kernels, local(): pl.pallas_call(body, out_shape=(jax.ShapeDtypeStruct((rows, width), bf16)...  114 us

commit v1 on v0

v1 whole, which is shorter than its diff:
```python
import functools

import jax
import jax.numpy as jnp
from jax import lax
from jax.experimental import pallas as pl
from jax.experimental.pallas import tpu as pltpu
from jax.sharding import PartitionSpec as P

ATOM_DEV = 32
CHUNKS = 4

inv_root_two = 0.7071067811865476
atom_scale = 0.2

MESH = pl.DeviceIdType.MESH
bf16 = jnp.bfloat16
f32 = jnp.float32


def scope(name):
    return jax.named_scope(name)


def silu(v):
    return v / (1.0 + jnp.exp(-v))


def flip(index, bit):
    return index + bit - 2 * bit * ((index // bit) % 2)


def one_hot(rows, ids):
    shape = (rows, ids.shape[1])
    return jnp.where(lax.broadcasted_iota(jnp.int32, shape, 0) == ids, 1.0, 0.0).astype(bf16)


def dot(a, b, ca=1, cb=0):
    return lax.dot_general(a, b, (((ca,), (cb,)), ((), ())), preferred_element_type=f32)


def halves(v):
    high = v.astype(bf16)
    return high, (v - high.astype(f32)).astype(bf16)


def gather_plan(mp):
    plan, held, bit = [], [0], mp // 2
    while bit >= 1:
        plan += [(bit, off) for off in held]
        held += [bit ^ off for off in held]
        bit //= 2
    return plan, held


def kernel(
    graph, mp, tile,
    state_hbm, down_hbm, basis_hbm, bw_hbm, up_hbm, dense_hbm, lists_hbm, in_hbm, out_hbm, live_hbm, atom_hbm,
    edge_out_ref, atom_out_ref,
    state_ref, down_ref, basis_ref, bw_ref, up_ref, lists_ref, in_ref, out_ref, live_ref, atom_ref, load_sem,
    weight, weight_sem,
    part_a, got_a, sum_a, more_a, full_a,
    part_b, got_b, sum_b, more_b, full_b,
    red_send, red_recv,
    to_a, from_a, to_b, from_b, xc_send, xc_recv,
    list_hot, basis_stack, bw_stack, angle, slots, in_hot, out_hot,
    acts, hidden, act_send, act_recv,
    atoms_own, atoms_to, atoms_from, table,
):
    g = lax.axis_index("graph")
    m = lax.axis_index("mp")
    rows, width = state_ref.shape
    trip = down_ref.shape[1]
    layers = weight.shape[0] // 2
    cap = lists_ref.shape[2]
    slot_total = graph * cap
    pieces, lane = to_a.shape[0], to_a.shape[2]
    kept = in_hot is not None
    triplets = in_ref.shape[1]
    atoms = graph * ATOM_DEV
    half = rows // 2
    bits = [1 << i for i in range(mp.bit_length() - 1)]
    stages = len(bits)
    size = rows // CHUNKS

    barrier = pltpu.get_barrier_semaphore()

    def greet(k, _):
        pl.semaphore_signal(barrier, inc=1, device_id={"graph": (g + k) % graph}, device_id_type=MESH)
        return 0

    lax.fori_loop(1, graph, greet, 0)
    for bit in bits:
        pl.semaphore_signal(barrier, inc=1, device_id={"mp": flip(m, bit)}, device_id_type=MESH)

    hbm = [state_hbm, down_hbm, lists_hbm, in_hbm, out_hbm, live_hbm, basis_hbm, bw_hbm, up_hbm, atom_hbm]
    here_refs = [state_ref, down_ref, lists_ref, in_ref, out_ref, live_ref, basis_ref, bw_ref, up_ref, atom_ref]
    loads = [pltpu.make_async_copy(a, b, load_sem.at[i]) for i, (a, b) in enumerate(zip(hbm, here_refs))]
    for load in loads:
        load.start()
    state_in, down_in, lists_in, in_in, out_in, live_in, basis_in, bw_in, up_in, atom_in = loads

    def mp_copy(src, dst, which, j, stage, bit):
        return pltpu.make_async_remote_copy(
            src_ref=src, dst_ref=dst, send_sem=red_send.at[which, j, stage], recv_sem=red_recv.at[which, j, stage],
            device_id={"mp": flip(m, bit)}, device_id_type=MESH)

    mine = pl.ds(pl.multiple_of((m % 2) * half, half), half)
    other = pl.ds(pl.multiple_of(half - (m % 2) * half, half), half)

    class Sum:
        def __init__(self, which, part, got, summed, more, full):
            self.which, self.part, self.got = which, part, got
            self.summed, self.more, self.full = summed, more, full

        def first(self, j):
            return mp_copy(self.part.at[j, other], self.got.at[j], self.which, j, 0, 1)

        def step(self, j, b):
            return mp_copy(self.summed.at[j, b], self.more.at[j, b], self.which, j, 1 + b, bits[1 + b])

        def last(self, j):
            at = self.full.at[j, mine]
            return mp_copy(at, at, self.which, j, stages, 1)

        def into(self, j):
            self.first(j).start()

        def across(self, j):
            self.first(j).wait_recv()
            total = self.part[j, mine].astype(f32) + self.got[j].astype(f32)
            if stages > 1:
                self.summed[j, 0] = total.astype(bf16)
                self.step(j, 0).start()
            else:
                self.full[j, mine] = total.astype(bf16)

        def home(self, j):
            for b in range(stages - 1):
                self.step(j, b).wait_recv()
                total = self.summed[j, b].astype(f32) + self.more[j, b].astype(f32)
                if b + 2 < stages:
                    self.summed[j, b + 1] = total.astype(bf16)
                    self.step(j, b + 1).start()
                else:
                    self.full[j, mine] = total.astype(bf16)
            self.last(j).start()

        def done(self, j):
            self.last(j).wait_recv()

        def drain(self):
            for j in range(pieces):
                self.first(j).wait_send()
                for b in range(stages - 1):
                    self.step(j, b).wait_send()
                self.last(j).wait_send()

    sum0 = Sum(0, part_a, got_a, sum_a, more_a, full_a)
    sum1 = Sum(1, part_b, got_b, sum_b, more_b, full_b)

    def exchange(which, src_at, dst_at, whole):
        def copy(k):
            peer = (g + k) % graph
            return pltpu.make_async_remote_copy(
                src_ref=src_at(peer), dst_ref=dst_at(g), send_sem=xc_send.at[which], recv_sem=xc_recv.at[which],
                device_id={"graph": peer}, device_id_type=MESH)

        def start(k, _):
            copy(k).start()
            return 0

        total = pltpu.make_async_remote_copy(
            src_ref=whole, dst_ref=whole, send_sem=xc_send.at[which], recv_sem=xc_recv.at[which],
            device_id={"graph": (g + 1) % graph}, device_id_type=MESH)
        return (lambda: lax.fori_loop(1, graph, start, 0)), total.wait_recv, total.wait_send

    def block(ref, size):
        return lambda i: ref.at[pl.ds(pl.multiple_of(i * size, size), size)]

    def piece(ref, j, size):
        return lambda i: ref.at[j, pl.ds(pl.multiple_of(i * size, size), size)]

    def tiles(step):
        def one(i, _):
            step(pl.ds(pl.multiple_of(i * tile, tile), tile))
            return 0

        lax.fori_loop(0, triplets // tile, one, 0)

    def in_part(at):
        return one_hot(slot_total, in_ref[:, at])

    def out_part(at):
        return one_hot(slot_total, jnp.where(live_ref[:, at] > 0, out_ref[:, at], -1))

    state_in.wait()
    down_in.wait()
    with scope("s_proj"):
        projected = dot(state_ref[...], down_ref[...]).astype(bf16)
        for j in range(pieces):
            part_a[j] = projected[:, j * lane:(j + 1) * lane]
    with scope("s_barrier"):
        pl.semaphore_wait(barrier, graph - 1 + len(bits))
    for j in range(pieces):
        sum0.into(j)
    load = pltpu.make_async_copy(dense_hbm, weight, weight_sem)
    load.start()

    lists_in.wait()
    with scope("s_hots"):
        for i in range(graph):
            list_hot[:, i * cap:(i + 1) * cap] = one_hot(rows, lists_ref[0, i:i + 1, :])
        in_in.wait()
        if kept:
            def keep_in(at):
                in_hot[:, at] = in_part(at)

            tiles(keep_in)
    with scope("s_across"):
        for j in range(pieces):
            sum0.across(j)
    out_in.wait()
    live_in.wait()
    if kept:
        def keep_out(at):
            out_hot[:, at] = out_part(at)

        with scope("s_outhot"):
            tiles(keep_out)

    basis_in.wait()
    bw_in.wait()
    depth = basis_ref.shape[0]
    pad = basis_stack.shape[0] // 3
    with scope("s_angles"):
        bw_high, bw_low = halves(bw_ref[...])
        bw_stack[...] = jnp.zeros_like(bw_stack)
        bw_stack[0:depth] = bw_high
        bw_stack[pad:pad + depth] = bw_high
        bw_stack[2 * pad:2 * pad + depth] = bw_low

        def angles(at):
            high, low = halves(basis_ref[:, at])
            basis_stack[:, at] = jnp.zeros((3 * pad, tile), bf16)
            basis_stack[0:depth, at] = high
            basis_stack[pad:pad + depth, at] = low
            basis_stack[2 * pad:2 * pad + depth, at] = high
            angle[:, at] = dot(bw_stack[...], basis_stack[:, at], 0, 0)

        tiles(angles)

    step_rows = min(slot_total, 512)
    own = pl.ds(pl.multiple_of(g * cap, cap), cap)
    span = pl.ds(0, slot_total - cap)
    going = [exchange(j, piece(to_a, j, cap), piece(from_a, j, cap), from_a.at[j, span]) for j in range(pieces)]
    back = [exchange(pieces + j, piece(to_b, j, cap), piece(from_b, j, cap), from_b.at[j, span])
            for j in range(pieces)]

    def pick_piece(j):
        def pick(i, _):
            at = pl.ds(pl.multiple_of(i * step_rows, step_rows), step_rows)
            to_a[j, at, :] = dot(list_hot[:, at], full_a[j], 0, 0).astype(bf16)
            return 0

        sum0.done(j)
        lax.fori_loop(0, slot_total // step_rows, pick, 0)
        going[j][0]()
        from_a[j, own] = to_a[j, own]

    with scope("s_home"):
        sum0.home(0)
    with scope("s_home1"):
        for j in range(1, pieces):
            sum0.home(j)
            pick_piece(j - 1)
        pick_piece(pieces - 1)
    sum0.drain()

    for j in range(pieces):
        with scope("s_gowait%d" % j):
            going[j][1]()
        slots[...] = jnp.zeros_like(slots)
        received = from_a[j].astype(f32).T.astype(bf16)

        def trips(at):
            source = in_hot[:, at] if kept else in_part(at)
            value = dot(received, source) * angle[j * lane:(j + 1) * lane, at]
            target = out_hot[:, at] if kept else out_part(at)
            slots[...] += dot(target, value.astype(bf16), 1, 1)

        with scope("s_trips%d" % j):
            tiles(trips)
        to_b[j] = slots[...].astype(bf16)
        back[j][0]()
        from_b[j, own] = to_b[j, own]

    up_in.wait()

    def add_up(j):
        rest = dot(full_b[j], up_ref[j * lane:(j + 1) * lane, :])
        hidden[...] = (state_ref[...].astype(f32) if j == 0 else hidden[...]) + rest

    for j in range(pieces):
        with scope("s_backwait%d" % j):
            back[j][1]()
        part_b[j] = dot(list_hot[...], from_b[j]).astype(bf16)
        sum1.into(j)
        if j + 1 < pieces:
            sum1.across(j)
    with scope("s_sum1"):
        if pieces > 1:
            sum1.home(0)
        sum1.across(pieces - 1)
        for j in range(1 if pieces > 1 else 0, pieces):
            sum1.home(j)
            if j >= 1:
                sum1.done(j - 1)
                add_up(j - 1)
        sum1.done(pieces - 1)

    plan, held = gather_plan(mp)
    order = [h * (CHUNKS // 2) + i for i in range(CHUNKS // 2) for h in (0, 1)]

    def other_of(off):
        index = m
        for bit in bits:
            if off & bit:
                index = flip(index, bit)
        return index

    def act_copy(layer, parity, c, which):
        bit, off = plan[which]
        at = acts.at[layer, other_of(off), pl.ds(c * size, size)]
        return pltpu.make_async_remote_copy(
            src_ref=at, dst_ref=at,
            send_sem=act_send.at[parity, c, which], recv_sem=act_recv.at[parity, c, which],
            device_id={"mp": flip(m, bit)}, device_id_type=MESH)

    local = [i for i, (bit, off) in enumerate(plan) if off == 0]
    relayed = [i for i, (bit, off) in enumerate(plan) if off != 0]
    brings = {bit ^ off: i for i, (bit, off) in enumerate(plan)}
    relays_from = sorted({brings[plan[i][1]] for i in relayed})

    def send(layer, parity, c):
        for i in local:
            act_copy(layer, parity, c, i).start()

    def relay(layer, parity, c):
        for i in relayed:
            first = brings[plan[i][1]]
            if [j for j in relayed if brings[plan[j][1]] == first][0] == i:
                act_copy(layer, parity, c, first).wait_recv()
            act_copy(layer, parity, c, i).start()

    def finish(layer, parity, c):
        for i in range(len(plan)):
            if i not in relays_from:
                act_copy(layer, parity, c, i).wait_recv()

    def sent(layer, parity, c):
        for i in range(len(plan)):
            act_copy(layer, parity, c, i).wait_send()

    last_up = (pieces - 1) * lane
    with scope("s_begin"):
        for c in order:
            at = pl.ds(c * size, size)
            before = hidden[at, :] if pieces > 1 else state_ref[at, :].astype(f32)
            first = before + dot(full_b[pieces - 1, at], up_ref[last_up:last_up + lane, :])
            hidden[at, :] = first
            acts[0, m, at, :] = first.astype(bf16)
            send(0, 0, c)
        sum1.drain()
        load.wait()
        for j in range(pieces):
            going[j][2]()
            back[j][2]()
    with scope("s_relay0"):
        relay(0, 0, order[0])

    def layer_step(l, _):
        for inside in range(2):
            k = 2 * l + inside
            for spot, c in enumerate(order):
                at = pl.ds(c * size, size)
                if spot + 1 < CHUNKS:
                    relay(k, inside, order[spot + 1])
                elif inside == 0:
                    relay(k + 1, 1, order[0])
                else:
                    @pl.when(l + 1 < layers)
                    def _():
                        relay(k + 1, 0, order[0])
                finish(k, inside, c)
                total = None
                for off in held:
                    index = other_of(off)
                    term = dot(acts[k, index, at, :], weight[k, pl.ds(pl.multiple_of(index * width, width), width), :])
                    total = term if total is None else total + term
                value = silu(total)
                if inside == 0:
                    @pl.when(l > 0)
                    def _():
                        sent(k - 1, 1, c)

                    acts[k + 1, m, at, :] = value.astype(bf16)
                    send(k + 1, 1, c)
                else:
                    value = (hidden[at, :] + value) * inv_root_two
                    hidden[at, :] = value

                    @pl.when(l + 1 < layers)
                    def _():
                        sent(k - 1, 0, c)
                        acts[k + 1, m, at, :] = value.astype(bf16)
                        send(k + 1, 0, c)
        return 0

    with scope("s_layers"):
        lax.fori_loop(0, layers, layer_step, 0)

    atom_in.wait()
    atom_rows = min(atoms, 256)

    def collect(i, _):
        at = pl.ds(pl.multiple_of(i * atom_rows, atom_rows), atom_rows)
        ids = one_hot(atom_rows, atom_ref[...] - i * atom_rows)
        high, low = halves(hidden[...])
        total = dot(ids, high) + dot(ids, low)
        atoms_own[at, :] = total
        atoms_to[at, :] = total.astype(bf16)
        return 0

    with scope("s_collect"):
        lax.fori_loop(0, atoms // atom_rows, collect, 0)
    atom_span = pl.ds(0, atoms - ATOM_DEV)
    start, wait, wait_sent = exchange(
        2 * pieces, block(atoms_to, ATOM_DEV), block(atoms_from, ATOM_DEV), atoms_from.at[atom_span])
    start()
    here = pl.ds(pl.multiple_of(g * ATOM_DEV, ATOM_DEV), ATOM_DEV)
    atoms_from[here] = jnp.zeros((ATOM_DEV, width), bf16)
    for c in range(CHUNKS):
        sent(2 * layers - 2, 0, c)
        sent(2 * layers - 1, 1, c)
    with scope("s_atomwait"):
        wait()

    def add(i, total):
        return total + atoms_from[pl.ds(pl.multiple_of(i * ATOM_DEV, ATOM_DEV), ATOM_DEV)].astype(f32)

    total = lax.fori_loop(0, graph, add, atoms_own[here])
    mine_out = silu(atom_scale * total).astype(bf16)
    table[here] = mine_out
    start2, wait2, wait_sent2 = exchange(
        2 * pieces + 1, lambda peer: block(table, ATOM_DEV)(g), block(table, ATOM_DEV), table.at[atom_span])
    start2()
    atom_out_ref[...] = mine_out
    wait_sent()
    with scope("s_atomwait2"):
        wait2()

    def spread(i, _):
        at = pl.ds(pl.multiple_of(i * atom_rows, atom_rows), atom_rows)
        hidden[...] += dot(one_hot(atom_rows, atom_ref[...] - i * atom_rows), table[at, :], 0, 0)
        return 0

    with scope("s_spread"):
        lax.fori_loop(0, atoms // atom_rows, spread, 0)
        edge_out_ref[...] = hidden[...].astype(bf16)
    wait_sent2()


def hand_on(edge_ref, atom_ref, edge_out_ref, atom_out_ref):
    edge_out_ref[...] = edge_ref[...]
    atom_out_ref[...] = atom_ref[...]


def local(graph, mp, edge_state, down_weight, basis, basis_weight, up_weight, dense_weight,
          send_rows, trip_in, trip_out, trip_live, edge_atom):
    rows, width = edge_state.shape
    trip = down_weight.shape[1]
    slot_total = graph * send_rows.shape[2]
    triplets = trip_in.shape[0]
    maps = dense_weight.shape[0] * dense_weight.shape[1]
    tile = 2048 if slot_total <= 512 else 128
    atoms = graph * ATOM_DEV
    stages = mp.bit_length()
    extra = max(stages - 2, 1)
    half = rows // 2
    vmem = pltpu.VMEM
    pieces = trip // 128 if trip % 128 == 0 else 1
    lane = trip // pieces
    pad = -(-basis.shape[0] // 16) * 16
    hot_bytes = 2 * 2 * slot_total * triplets
    hots = [vmem((slot_total, triplets), bf16)] * 2 if hot_bytes <= 2 ** 24 else [None, None]
    reduce_bufs = [
        vmem((pieces, rows, lane), bf16), vmem((pieces, half, lane), bf16), vmem((pieces, extra, half, lane), bf16),
        vmem((pieces, extra, half, lane), bf16), vmem((pieces, rows, lane), bf16),
    ]
    dma = pltpu.SemaphoreType.DMA
    spec = pl.BlockSpec(memory_space=pltpu.VMEM)
    operands = [
        edge_state, down_weight, basis, basis_weight, up_weight,
        dense_weight.reshape((maps,) + dense_weight.shape[2:]),
        send_rows, trip_in.reshape(1, triplets), trip_out.reshape(1, triplets),
        trip_live.reshape(1, triplets), edge_atom.reshape(1, rows),
    ]
    inputs = [vmem(a.shape, a.dtype) for i, a in enumerate(operands) if i != 5]
    body = functools.partial(kernel, graph, mp, tile)
    before = [
        *inputs, dma((len(inputs),)),
        vmem((maps,) + dense_weight.shape[2:], bf16), dma(()),
        *reduce_bufs, *reduce_bufs,
        dma((2, pieces, stages)), dma((2, pieces, stages)),
        *[vmem((pieces, slot_total, lane), bf16)] * 4,
        dma((2 * pieces + 2,)), dma((2 * pieces + 2,)),
        vmem((rows, slot_total), bf16), vmem((3 * pad, triplets), bf16), vmem((3 * pad, trip), bf16),
        vmem((trip, triplets), f32), vmem((slot_total, lane), f32),
    ]
    if hots[0] is None:
        hots, kept_body, at = [], body, len(operands) + 2 + len(before)
        body = lambda *refs: kept_body(*refs[:at], None, None, *refs[at:])
    outs = pl.pallas_call(
        body,
        out_shape=(
            jax.ShapeDtypeStruct((rows, width), bf16),
            jax.ShapeDtypeStruct((ATOM_DEV, width), bf16),
        ),
        in_specs=[pl.BlockSpec(memory_space=pl.ANY)] * len(operands),
        out_specs=(spec, spec),
        scratch_shapes=[
            *before, *hots,
            vmem((maps, mp, rows, width), bf16), vmem((rows, width), f32),
            dma((2, CHUNKS, mp - 1)), dma((2, CHUNKS, mp - 1)),
            vmem((atoms, width), f32), vmem((atoms, width), bf16), vmem((atoms, width), bf16),
            vmem((atoms, width), bf16),
        ],
        compiler_params=pltpu.CompilerParams(
            collective_id=0, has_side_effects=True, vmem_limit_bytes=64000 * 1024
        ),
        name="edge_block",
    )(*operands)
    return pl.pallas_call(
        hand_on,
        out_shape=tuple(jax.ShapeDtypeStruct(o.shape, o.dtype) for o in outs),
        in_specs=[spec] * 2,
        out_specs=(spec, spec),
        name="hand_on",
    )(*outs)


def solution(mesh):
    in_specs = (
        P("graph", "mp"),
        P("mp", None),
        P(None, ("graph", "mp")),
        P(),
        P(None, "mp"),
        P(None, None, None, "mp"),
        P("graph", "mp", None),
        P(("graph", "mp")),
        P(("graph", "mp")),
        P(("graph", "mp")),
        P("graph"),
    )
    out_specs = (P("graph", "mp"), P("graph", "mp"))
    body = functools.partial(local, mesh.shape["graph"], mesh.shape["mp"])
    return jax.shard_map(body, mesh=mesh, in_specs=in_specs, out_specs=out_specs, check_vma=False)
```

time: 116 us -> 109 us (0.940)
  Pallas kernels: 115 us -> 108 us
    pallas_call x1, Pallas kernels: 114 us -> 106 us  [local(): pl.pallas_call(body, out_shape=(jax.ShapeDtypeStruct((rows, width), bf16)...]
where the time goes in v1:
time: 109 us
  Pallas kernels  108 us (99%)
    pallas_call x1, Pallas kernels, local(): pl.pallas_call(body, out_shape=(jax.ShapeDtypeStruct((rows, width), bf16)...  106 us

profile of v1, /device:TPU:0, one launch (start us, length us, event | category | flops | bytes accessed | tf_op | source)
XLA Modules:
  0.0 108.6 jit_solution(11036889663761402363)
XLA Ops:
  0.6 106.2 %edge_block.1 = (bf16[512,384]{1,0:T(8,128)(2,1)}, bf16[32,384]{1,0:T(8,128)(2,1)}) custom-call(bf16[512,384]{1,0:T(8,128)(2,1)} %state_hbm.1, bf16[384,384]{1,0:T(8,128)(2,1)} %down_hbm.1, f32[42,4096]{1,0:T(8,128)} %basis_hbm.1, f32[42,384]{1,0:T(8,128)} %bw_hbm.1, bf16[384,384]{1,0:T(8,128)(2,1)} %up_hbm.1, bf16[6,1536,384]{2,1,0:T(8,128)(2,1)} %bitcast.5, ...), custom_call_target="tpu_custom_call" | custom-call | tf_op jit(solution)/shard_map/edge_block/pallas_call | solution.py:524
  106.8 1.8 %hand_on.1 = (bf16[512,384]{1,0:T(8,128)(2,1)}, bf16[32,384]{1,0:T(8,128)(2,1)}) custom-call(bf16[512,384]{1,0:T(8,128)(2,1)} %get-tuple-element.4.edge_ref, bf16[32,384]{1,0:T(8,128)(2,1)} %get-tuple-element.5.atom_ref), custom_call_target="tpu_custom_call" | custom-call | tf_op jit(solution)/shard_map/hand_on/pallas_call | solution.py:544

commit v2 on v1

--- a/solution.py
+++ b/solution.py
@@ -57,19 +57,20 @@
     graph, mp, tile,
     state_hbm, down_hbm, basis_hbm, bw_hbm, up_hbm, dense_hbm, lists_hbm, in_hbm, out_hbm, live_hbm, atom_hbm,
     edge_out_ref, atom_out_ref,
-    state_ref, down_ref, basis_ref, bw_ref, up_ref, lists_ref, in_ref, out_ref, live_ref, atom_ref, load_sem,
+    down_ref, basis_ref, bw_ref, lists_ref, in_ref, out_ref, live_ref, atom_ref, load_sem,
+    states, ups, early_send, early_recv,
     weight, weight_sem,
     part_a, got_a, sum_a, more_a, full_a,
     part_b, got_b, sum_b, more_b, full_b,
     red_send, red_recv,
     to_a, from_a, to_b, from_b, xc_send, xc_recv,
     list_hot, basis_stack, bw_stack, angle, slots, in_hot, out_hot,
-    acts, hidden, act_send, act_recv,
+    acts, partial, hidden, act_send, act_recv,
     atoms_own, atoms_to, atoms_from, table,
 ):
     g = lax.axis_index("graph")
     m = lax.axis_index("mp")
-    rows, width = state_ref.shape
+    rows, width = hidden.shape
     trip = down_ref.shape[1]
     layers = weight.shape[0] // 2
     cap = lists_ref.shape[2]
@@ -94,7 +95,8 @@
         pl.semaphore_signal(barrier, inc=1, device_id={"mp": flip(m, bit)}, device_id_type=MESH)
 
     hbm = [state_hbm, down_hbm, lists_hbm, in_hbm, out_hbm, live_hbm, basis_hbm, bw_hbm, up_hbm, atom_hbm]
-    here_refs = [state_ref, down_ref, lists_ref, in_ref, out_ref, live_ref, basis_ref, bw_ref, up_ref, atom_ref]
+    here_refs = [
+        states.at[m], down_ref, lists_ref, in_ref, out_ref, live_ref, basis_ref, bw_ref, ups.at[m], atom_ref]
     loads = [pltpu.make_async_copy(a, b, load_sem.at[i]) for i, (a, b) in enumerate(zip(hbm, here_refs))]
     for load in loads:
         load.start()
@@ -107,6 +109,39 @@
 
     mine = pl.ds(pl.multiple_of((m % 2) * half, half), half)
     other = pl.ds(pl.multiple_of(half - (m % 2) * half, half), half)
+
+    plan, held = gather_plan(mp)
+
+    def other_of(off):
+        index = m
+        for bit in bits:
+            if off & bit:
+                index = flip(index, bit)
+        return index
+
+    local = [i for i, (bit, off) in enumerate(plan) if off == 0]
+    relayed = [i for i, (bit, off) in enumerate(plan) if off != 0]
+    brings = {bit ^ off: i for i, (bit, off) in enumerate(plan)}
+    relays_from = sorted({brings[plan[i][1]] for i in relayed})
+
+    def early(which, i):
+        bit, off = plan[i]
+        at = (states, ups)[which].at[other_of(off)]
+        return pltpu.make_async_remote_copy(
+            src_ref=at, dst_ref=at, send_sem=early_send.at[which, i], recv_sem=early_recv.at[which, i],
+            device_id={"mp": flip(m, bit)}, device_id_type=MESH)
+
+    def early_relay(which):
+        for i in relayed:
+            first = brings[plan[i][1]]
+            if [j for j in relayed if brings[plan[j][1]] == first][0] == i:
+                early(which, first).wait_recv()
+            early(which, i).start()
+
+    def early_finish(which):
+        for i in range(len(plan)):
+            if i not in relays_from:
+                early(which, i).wait_recv()
 
     class Sum:
         def __init__(self, which, part, got, summed, more, full):
@@ -197,7 +232,7 @@
     state_in.wait()
     down_in.wait()
     with scope("s_proj"):
-        projected = dot(state_ref[...], down_ref[...]).astype(bf16)
+        projected = dot(states[m], down_ref[...]).astype(bf16)
         for j in range(pieces):
             part_a[j] = projected[:, j * lane:(j + 1) * lane]
     with scope("s_barrier"):
@@ -220,6 +255,10 @@
     with scope("s_across"):
         for j in range(pieces):
             sum0.across(j)
+    up_in.wait()
+    for which in range(2):
+        for i in local[:1]:
+            early(which, i).start()
     out_in.wait()
     live_in.wait()
     if kept:
@@ -275,6 +314,9 @@
             sum0.home(j)
             pick_piece(j - 1)
         pick_piece(pieces - 1)
+    for which in range(2):
+        for i in local[1:]:
+            early(which, i).start()
     sum0.drain()
 
     for j in range(pieces):
@@ -294,24 +336,30 @@
         to_b[j] = slots[...].astype(bf16)
         back[j][0]()
         from_b[j, own] = to_b[j, own]
-
-    up_in.wait()
+    with scope("s_early0"):
+        early_relay(0)
 
     def add_up(j):
-        rest = dot(full_b[j], up_ref[j * lane:(j + 1) * lane, :])
-        hidden[...] = (state_ref[...].astype(f32) if j == 0 else hidden[...]) + rest
+        for index in range(mp):
+            rest = dot(full_b[j], ups[index, j * lane:(j + 1) * lane, :])
+            partial[index] = (states[index].astype(f32) if j == 0 else partial[index]) + rest
 
     for j in range(pieces):
         with scope("s_backwait%d" % j):
             back[j][1]()
         part_b[j] = dot(list_hot[...], from_b[j]).astype(bf16)
         sum1.into(j)
+        if j == 0:
+            with scope("s_early1"):
+                early_relay(1)
         if j + 1 < pieces:
             sum1.across(j)
     with scope("s_sum1"):
         if pieces > 1:
             sum1.home(0)
         sum1.across(pieces - 1)
+        early_finish(0)
+        early_finish(1)
         for j in range(1 if pieces > 1 else 0, pieces):
             sum1.home(j)
             if j >= 1:
@@ -319,15 +367,7 @@
                 add_up(j - 1)
         sum1.done(pieces - 1)
 
-    plan, held = gather_plan(mp)
     order = [h * (CHUNKS // 2) + i for i in range(CHUNKS // 2) for h in (0, 1)]
-
-    def other_of(off):
-        index = m
-        for bit in bits:
-            if off & bit:
-                index = flip(index, bit)
-        return index
 
     def act_copy(layer, parity, c, which):
         bit, off = plan[which]
@@ -337,11 +377,6 @@
             send_sem=act_send.at[parity, c, which], recv_sem=act_recv.at[parity, c, which],
             device_id={"mp": flip(m, bit)}, device_id_type=MESH)
 
-    local = [i for i, (bit, off) in enumerate(plan) if off == 0]
-    relayed = [i for i, (bit, off) in enumerate(plan) if off != 0]
-    brings = {bit ^ off: i for i, (bit, off) in enumerate(plan)}
-    relays_from = sorted({brings[plan[i][1]] for i in relayed})
-
     def send(layer, parity, c):
         for i in local:
             act_copy(layer, parity, c, i).start()
@@ -362,118 +397,142 @@
         for i in range(len(plan)):
             act_copy(layer, parity, c, i).wait_send()
 
+    def product(k, at):
+        total = None
+        for off in held:
+            index = other_of(off)
+            term = dot(acts[k, index, at, :], weight[k, pl.ds(pl.multiple_of(index * width, width), width), :])
+            total = term if total is None else total + term
+        return silu(total)
+
     last_up = (pieces - 1) * lane
+    load.wait()
     with scope("s_begin"):
         for c in order:
             at = pl.ds(c * size, size)
-            before = hidden[at, :] if pieces > 1 else state_ref[at, :].astype(f32)
-            first = before + dot(full_b[pieces - 1, at], up_ref[last_up:last_up + lane, :])
-            hidden[at, :] = first
-            acts[0, m, at, :] = first.astype(bf16)
-            send(0, 0, c)
+            for index in range(mp):
+                before = partial[index, at] if pieces > 1 else states[index, at].astype(f32)
+                first = before + dot(full_b[pieces - 1, at], ups[index, last_up:last_up + lane, :])
+                partial[index, at] = first
+                acts[0, index, at, :] = first.astype(bf16)
+            hidden[at, :] = partial[m, at]
+            acts[1, m, at, :] = product(0, at).astype(bf16)
+            send(1, 1, c)
         sum1.drain()
-        load.wait()
         for j in range(pieces):
             going[j][2]()
             back[j][2]()
-    with scope("s_relay0"):
-        relay(0, 0, order[0])
+        for which in range(2):
+            for i in range(len(plan)):
+                early(which, i).wait_send()
+    with scope("s_relay1"):
+        relay(1, 1, order[0])
+
+    def half_step(l, inside, first):
+        k = 2 * l + inside
+        for spot, c in enumerate(order):
+            at = pl.ds(c * size, size)
+            if spot + 1 < CHUNKS:
+                relay(k, inside, order[spot + 1])
+            elif inside == 0:
+                relay(k + 1, 1, order[0])
+            elif not first or layers > 1:
+                @pl.when(l + 1 < layers)
+                def _():
+                    relay(k + 1, 0, order[0])
+            finish(k, inside, c)
+            value = product(k, at)
+            if inside == 0:
+                sent(k - 1, 1, c)
+                acts[k + 1, m, at, :] = value.astype(bf16)
+                send(k + 1, 1, c)
+            else:
+                value = (hidden[at, :] + value) * inv_root_two
+                hidden[at, :] = value
+
+                @pl.when(l + 1 < layers)
+                def _():
+                    if not first:
+                        sent(k - 1, 0, c)
+                    acts[k + 1, m, at, :] = value.astype(bf16)
+                    send(k + 1, 0, c)
 
     def layer_step(l, _):
-        for inside in range(2):
-            k = 2 * l + inside
-            for spot, c in enumerate(order):
-                at = pl.ds(c * size, size)
-                if spot + 1 < CHUNKS:
-                    relay(k, inside, order[spot + 1])
-                elif inside == 0:
-                    relay(k + 1, 1, order[0])
-                else:
-                    @pl.when(l + 1 < layers)
-                    def _():
-                        relay(k + 1, 0, order[0])
-                finish(k, inside, c)
-                total = None
-                for off in held:
-                    index = other_of(off)
-                    term = dot(acts[k, index, at, :], weight[k, pl.ds(pl.multiple_of(index * width, width), width), :])
-                    total = term if total is None else total + term
-                value = silu(total)
-                if inside == 0:
-                    @pl.when(l > 0)
-                    def _():
-                        sent(k - 1, 1, c)
-
-                    acts[k + 1, m, at, :] = value.astype(bf16)
-                    send(k + 1, 1, c)
-                else:
-                    value = (hidden[at, :] + value) * inv_root_two
-                    hidden[at, :] = value
-
-                    @pl.when(l + 1 < layers)
-                    def _():
-                        sent(k - 1, 0, c)
-                        acts[k + 1, m, at, :] = value.astype(bf16)
-                        send(k + 1, 0, c)
+        half_step(l, 0, False)
+        half_step(l, 1, False)
         return 0
 
     with scope("s_layers"):
-        lax.fori_loop(0, layers, layer_step, 0)
+        half_step(0, 1, True)
+        lax.fori_loop(1, layers, layer_step, 0)
 
     atom_in.wait()
     atom_rows = min(atoms, 256)
-
-    def collect(i, _):
-        at = pl.ds(pl.multiple_of(i * atom_rows, atom_rows), atom_rows)
-        ids = one_hot(atom_rows, atom_ref[...] - i * atom_rows)
-        high, low = halves(hidden[...])
-        total = dot(ids, high) + dot(ids, low)
-        atoms_own[at, :] = total
-        atoms_to[at, :] = total.astype(bf16)
-        return 0
+    parts, part_lane = table.shape[0], table.shape[2]
+    here = pl.ds(pl.multiple_of(g * ATOM_DEV, ATOM_DEV), ATOM_DEV)
+    atom_span = pl.ds(0, atoms - ATOM_DEV)
+    gathers = [exchange(2 * pieces + p, piece(atoms_to, p, ATOM_DEV), piece(atoms_from, p, ATOM_DEV),
+                        atoms_from.at[p, atom_span]) for p in range(parts)]
+    spreads = [exchange(2 * pieces + parts + p, lambda peer, p=p: piece(table, p, ATOM_DEV)(g),
+                        piece(table, p, ATOM_DEV), table.at[p, atom_span]) for p in range(parts)]
+
+    def columns(p):
+        return slice(p * part_lane, (p + 1) * part_lane)
 
     with scope("s_collect"):
-        lax.fori_loop(0, atoms // atom_rows, collect, 0)
-    atom_span = pl.ds(0, atoms - ATOM_DEV)
-    start, wait, wait_sent = exchange(
-        2 * pieces, block(atoms_to, ATOM_DEV), block(atoms_from, ATOM_DEV), atoms_from.at[atom_span])
-    start()
-    here = pl.ds(pl.multiple_of(g * ATOM_DEV, ATOM_DEV), ATOM_DEV)
-    atoms_from[here] = jnp.zeros((ATOM_DEV, width), bf16)
+        for p in range(parts):
+            def collect(i, _):
+                at = pl.ds(pl.multiple_of(i * atom_rows, atom_rows), atom_rows)
+                ids = one_hot(atom_rows, atom_ref[...] - i * atom_rows)
+                high, low = halves(hidden[:, columns(p)])
+                total = dot(ids, high) + dot(ids, low)
+                atoms_own[p, at] = total
+                atoms_to[p, at] = total.astype(bf16)
+                return 0
+
+            lax.fori_loop(0, atoms // atom_rows, collect, 0)
+            gathers[p][0]()
+    for p in range(parts):
+        atoms_from[p, here] = jnp.zeros((ATOM_DEV, part_lane), bf16)
     for c in range(CHUNKS):
-        sent(2 * layers - 2, 0, c)
+        if layers > 1:
+            sent(2 * layers - 2, 0, c)
         sent(2 * layers - 1, 1, c)
-    with scope("s_atomwait"):
-        wait()
-
-    def add(i, total):
-        return total + atoms_from[pl.ds(pl.multiple_of(i * ATOM_DEV, ATOM_DEV), ATOM_DEV)].astype(f32)
-
-    total = lax.fori_loop(0, graph, add, atoms_own[here])
-    mine_out = silu(atom_scale * total).astype(bf16)
-    table[here] = mine_out
-    start2, wait2, wait_sent2 = exchange(
-        2 * pieces + 1, lambda peer: block(table, ATOM_DEV)(g), block(table, ATOM_DEV), table.at[atom_span])
-    start2()
-    atom_out_ref[...] = mine_out
-    wait_sent()
-    with scope("s_atomwait2"):
-        wait2()
-
-    def spread(i, _):
-        at = pl.ds(pl.multiple_of(i * atom_rows, atom_rows), atom_rows)
-        hidden[...] += dot(one_hot(atom_rows, atom_ref[...] - i * atom_rows), table[at, :], 0, 0)
-        return 0
-
-    with scope("s_spread"):
-        lax.fori_loop(0, atoms // atom_rows, spread, 0)
-        edge_out_ref[...] = hidden[...].astype(bf16)
-    wait_sent2()
-
-
-def hand_on(edge_ref, atom_ref, edge_out_ref, atom_out_ref):
-    edge_out_ref[...] = edge_ref[...]
-    atom_out_ref[...] = atom_ref[...]
+    for p in range(parts):
+        with scope("s_atomwait%d" % p):
+            gathers[p][1]()
+
+        def add(i, total):
+            return total + atoms_from[p, pl.ds(pl.multiple_of(i * ATOM_DEV, ATOM_DEV), ATOM_DEV)].astype(f32)
+
+        total = lax.fori_loop(0, graph, add, atoms_own[p, here])
+        mine_out = silu(atom_scale * total).astype(bf16)
+        table[p, here] = mine_out
+        spreads[p][0]()
+        atom_out_ref[:, columns(p)] = mine_out
+    for p in range(parts):
+        gathers[p][2]()
+    for p in range(parts):
+        with scope("s_spreadwait%d" % p):
+            spreads[p][1]()
+
+        def spread(i, total):
+            at = pl.ds(pl.multiple_of(i * atom_rows, atom_rows), atom_rows)
+            return total + dot(one_hot(atom_rows, atom_ref[...] - i * atom_rows), table[p, at], 0, 0)
+
+        total = lax.fori_loop(0, atoms // atom_rows, spread, hidden[:, columns(p)])
+        edge_out_ref[:, columns(p)] = total.astype(bf16)
+    for p in range(parts):
+        spreads[p][2]()
+
+
+def hand_on(edge_ref, atom_ref, edge_out_ref, atom_out_ref, sem):
+    edge = pltpu.make_async_copy(edge_ref, edge_out_ref, sem.at[0])
+    atom = pltpu.make_async_copy(atom_ref, atom_out_ref, sem.at[1])
+    edge.start()
+    atom.start()
+    edge.wait()
+    atom.wait()
 
 
 def local(graph, mp, edge_state, down_weight, basis, basis_weight, up_weight, dense_weight,
@@ -506,15 +565,18 @@
         send_rows, trip_in.reshape(1, triplets), trip_out.reshape(1, triplets),
         trip_live.reshape(1, triplets), edge_atom.reshape(1, rows),
     ]
-    inputs = [vmem(a.shape, a.dtype) for i, a in enumerate(operands) if i != 5]
+    inputs = [vmem(a.shape, a.dtype) for i, a in enumerate(operands) if i not in (0, 4, 5)]
+    parts = width // 128 if width % 128 == 0 else 1
+    atom_buf = (parts, atoms, width // parts)
     body = functools.partial(kernel, graph, mp, tile)
     before = [
-        *inputs, dma((len(inputs),)),
+        *inputs, dma((len(inputs) + 2,)),
+        vmem((mp, rows, width), bf16), vmem((mp, trip, width), bf16), dma((2, mp - 1)), dma((2, mp - 1)),
         vmem((maps,) + dense_weight.shape[2:], bf16), dma(()),
         *reduce_bufs, *reduce_bufs,
         dma((2, pieces, stages)), dma((2, pieces, stages)),
         *[vmem((pieces, slot_total, lane), bf16)] * 4,
-        dma((2 * pieces + 2,)), dma((2 * pieces + 2,)),
+        dma((2 * pieces + 2 * parts,)), dma((2 * pieces + 2 * parts,)),
         vmem((rows, slot_total), bf16), vmem((3 * pad, triplets), bf16), vmem((3 * pad, trip), bf16),
         vmem((trip, triplets), f32), vmem((slot_total, lane), f32),
     ]
@@ -524,28 +586,29 @@
     outs = pl.pallas_call(
         body,
         out_shape=(
-            jax.ShapeDtypeStruct((rows, width), bf16),
-            jax.ShapeDtypeStruct((ATOM_DEV, width), bf16),
+            pltpu.VMEM((rows, width), bf16),
+            pltpu.VMEM((ATOM_DEV, width), bf16),
         ),
         in_specs=[pl.BlockSpec(memory_space=pl.ANY)] * len(operands),
         out_specs=(spec, spec),
         scratch_shapes=[
             *before, *hots,
-            vmem((maps, mp, rows, width), bf16), vmem((rows, width), f32),
+            vmem((maps, mp, rows, width), bf16), vmem((mp, rows, width), f32), vmem((rows, width), f32),
             dma((2, CHUNKS, mp - 1)), dma((2, CHUNKS, mp - 1)),
-            vmem((atoms, width), f32), vmem((atoms, width), bf16), vmem((atoms, width), bf16),
-            vmem((atoms, width), bf16),
+            vmem(atom_buf, f32), vmem(atom_buf, bf16), vmem(atom_buf, bf16), vmem(atom_buf, bf16),
         ],
         compiler_params=pltpu.CompilerParams(
             collective_id=0, has_side_effects=True, vmem_limit_bytes=64000 * 1024
         ),
         name="edge_block",
     )(*operands)
+    outs = [pltpu.with_memory_space_constraint(o, pltpu.VMEM) for o in outs]
     return pl.pallas_call(
         hand_on,
         out_shape=tuple(jax.ShapeDtypeStruct(o.shape, o.dtype) for o in outs),
         in_specs=[spec] * 2,
-        out_specs=(spec, spec),
+        out_specs=[pl.BlockSpec(memory_space=pl.ANY)] * 2,
+        scratch_shapes=[dma((2,))],
         name="hand_on",
     )(*outs)
 

time: 109 us -> 99.4 us (0.912)
  Pallas kernels: 108 us -> 98.5 us
    pallas_call x1, Pallas kernels: 106 us -> 97.7 us  [local(): pl.pallas_call(body, out_shape=(pltpu.VMEM((rows, width), bf16), pltpu.VM...]
where the time goes in v2:
time: 99.4 us; the launch traced here: 99.3 us
  Pallas kernels  98.5 us (99%)
    pallas_call x1, Pallas kernels, local(): pl.pallas_call(body, out_shape=(pltpu.VMEM((rows, width), bf16), pltpu.VM...  97.7 us

profile of v2, /device:TPU:0, one launch (start us, length us, event | category | flops | bytes accessed | tf_op | source)
XLA Modules:
  0.0 99.3 jit_solution(9075679797974302572)
XLA Ops:
  0.6 97.7 %edge_block.1 = (bf16[512,384]{1,0:T(8,128)(2,1)S(1)}, bf16[32,384]{1,0:T(8,128)(2,1)S(1)}) custom-call(bf16[512,384]{1,0:T(8,128)(2,1)} %state_hbm.1, bf16[384,384]{1,0:T(8,128)(2,1)} %down_hbm.1, f32[42,4096]{1,0:T(8,128)} %basis_hbm.1, f32[42,384]{1,0:T(8,128)} %bw_hbm.1, bf16[384,384]{1,0:T(8,128)(2,1)} %up_hbm.1, bf16[6,1536,384]{2,1,0:T(8,128)(2,1)} %bitcast.5, ...), custom_call_target="tpu_custom_call" | custom-call | tf_op jit(solution)/shard_map/edge_block/pallas_call | solution.py:586
  98.3 0.8 hand_on.1

commit v3 on v2

--- a/solution.py
+++ b/solution.py
@@ -8,7 +8,6 @@
 from jax.sharding import PartitionSpec as P
 
 ATOM_DEV = 32
-CHUNKS = 4
 
 inv_root_two = 0.7071067811865476
 atom_scale = 0.2
@@ -42,6 +41,11 @@
 def halves(v):
     high = v.astype(bf16)
     return high, (v - high.astype(f32)).astype(bf16)
+
+
+def chunks_of(half):
+    quarter = half // 4
+    return (0, quarter, 3 * quarter), (quarter, 2 * quarter, quarter)
 
 
 def gather_plan(mp):
@@ -82,7 +86,6 @@
     half = rows // 2
     bits = [1 << i for i in range(mp.bit_length() - 1)]
     stages = len(bits)
-    size = rows // CHUNKS
 
     barrier = pltpu.get_barrier_semaphore()
 
@@ -104,7 +107,7 @@
 
     def mp_copy(src, dst, which, j, stage, bit):
         return pltpu.make_async_remote_copy(
-            src_ref=src, dst_ref=dst, send_sem=red_send.at[which, j, stage], recv_sem=red_recv.at[which, j, stage],
+            src_ref=src, dst_ref=dst, send_sem=red_send.at[which, stage], recv_sem=red_recv.at[which, j, stage],
             device_id={"mp": flip(m, bit)}, device_id_type=MESH)
 
     mine = pl.ds(pl.multiple_of((m % 2) * half, half), half)
@@ -128,8 +131,14 @@
         bit, off = plan[i]
         at = (states, ups)[which].at[other_of(off)]
         return pltpu.make_async_remote_copy(
-            src_ref=at, dst_ref=at, send_sem=early_send.at[which, i], recv_sem=early_recv.at[which, i],
+            src_ref=at, dst_ref=at, send_sem=early_send.at[which], recv_sem=early_recv.at[which, i],
             device_id={"mp": flip(m, bit)}, device_id_type=MESH)
+
+    def early_sent(which):
+        at = (states, ups)[which].at[pl.ds(0, mp - 1)]
+        pltpu.make_async_remote_copy(
+            src_ref=at, dst_ref=at, send_sem=early_send.at[which], recv_sem=early_recv.at[which, 0],
+            device_id={"mp": flip(m, 1)}, device_id_type=MESH).wait_send()
 
     def early_relay(which):
         for i in relayed:
@@ -185,30 +194,42 @@
             self.last(j).wait_recv()
 
         def drain(self):
-            for j in range(pieces):
-                self.first(j).wait_send()
-                for b in range(stages - 1):
-                    self.step(j, b).wait_send()
-                self.last(j).wait_send()
+            for stage in range(stages + 1):
+                mp_copy(self.got, self.got, self.which, 0, stage, 1).wait_send()
 
     sum0 = Sum(0, part_a, got_a, sum_a, more_a, full_a)
     sum1 = Sum(1, part_b, got_b, sum_b, more_b, full_b)
 
-    def exchange(which, src_at, dst_at, whole):
-        def copy(k):
-            peer = (g + k) % graph
-            return pltpu.make_async_remote_copy(
-                src_ref=src_at(peer), dst_ref=dst_at(g), send_sem=xc_send.at[which], recv_sem=xc_recv.at[which],
-                device_id={"graph": peer}, device_id_type=MESH)
-
-        def start(k, _):
-            copy(k).start()
+    def peer_of(k):
+        if graph & (graph - 1):
+            return (g + k) % graph
+        return sum(bit * ((g // bit + k // bit) % 2) for bit in (1 << i for i in range(graph.bit_length() - 1)))
+
+    peers = [peer_of(k) for k in range(graph - 1, 0, -1)] if graph <= 8 else None
+
+    def arrived(whole, group, which):
+        return pltpu.make_async_remote_copy(
+            src_ref=whole, dst_ref=whole, send_sem=xc_send.at[group], recv_sem=xc_recv.at[which],
+            device_id={"graph": (g + 1) % graph}, device_id_type=MESH)
+
+    def exchange(group, which, src_at, dst_at, whole):
+        def to(peer):
+            pltpu.make_async_remote_copy(
+                src_ref=src_at(peer), dst_ref=dst_at(g), send_sem=xc_send.at[group], recv_sem=xc_recv.at[which],
+                device_id={"graph": peer}, device_id_type=MESH).start()
+
+        def one(i, _):
+            to(peer_of(graph - 1 - i))
             return 0
 
-        total = pltpu.make_async_remote_copy(
-            src_ref=whole, dst_ref=whole, send_sem=xc_send.at[which], recv_sem=xc_recv.at[which],
-            device_id={"graph": (g + 1) % graph}, device_id_type=MESH)
-        return (lambda: lax.fori_loop(1, graph, start, 0)), total.wait_recv, total.wait_send
+        def start():
+            if peers is None:
+                lax.fori_loop(0, graph - 1, one, 0)
+            else:
+                for peer in peers:
+                    to(peer)
+
+        return start, arrived(whole, group, which).wait_recv
 
     def block(ref, size):
         return lambda i: ref.at[pl.ds(pl.multiple_of(i * size, size), size)]
@@ -292,8 +313,8 @@
     step_rows = min(slot_total, 512)
     own = pl.ds(pl.multiple_of(g * cap, cap), cap)
     span = pl.ds(0, slot_total - cap)
-    going = [exchange(j, piece(to_a, j, cap), piece(from_a, j, cap), from_a.at[j, span]) for j in range(pieces)]
-    back = [exchange(pieces + j, piece(to_b, j, cap), piece(from_b, j, cap), from_b.at[j, span])
+    going = [exchange(0, j, piece(to_a, j, cap), piece(from_a, j, cap), from_a.at[j, span]) for j in range(pieces)]
+    back = [exchange(1, pieces + j, piece(to_b, j, cap), piece(from_b, j, cap), from_b.at[j, span])
             for j in range(pieces)]
 
     def pick_piece(j):
@@ -355,26 +376,36 @@
         if j + 1 < pieces:
             sum1.across(j)
     with scope("s_sum1"):
-        if pieces > 1:
-            sum1.home(0)
+        for j in range(pieces - 2):
+            sum1.home(j)
         sum1.across(pieces - 1)
         early_finish(0)
         early_finish(1)
-        for j in range(1 if pieces > 1 else 0, pieces):
-            sum1.home(j)
-            if j >= 1:
-                sum1.done(j - 1)
-                add_up(j - 1)
-        sum1.done(pieces - 1)
-
-    order = [h * (CHUNKS // 2) + i for i in range(CHUNKS // 2) for h in (0, 1)]
+        if pieces > 1:
+            sum1.home(pieces - 2)
+        for j in range(pieces - 1):
+            sum1.done(j)
+            add_up(j)
+        with scope("s_lasthome"):
+            sum1.home(pieces - 1)
+
+    starts, sizes = chunks_of(half)
+    order = [(h, t) for t in range(len(sizes)) for h in (0, 1)]
+
+    def chunk(c):
+        side, t = c
+        start = side * half + starts[t]
+        return pl.ds(start if isinstance(side, int) else pl.multiple_of(start, half // 4), sizes[t])
+
+    def chunk_id(c):
+        return c[0] * len(sizes) + c[1]
 
     def act_copy(layer, parity, c, which):
         bit, off = plan[which]
-        at = acts.at[layer, other_of(off), pl.ds(c * size, size)]
+        at = acts.at[layer, other_of(off), chunk(c)]
         return pltpu.make_async_remote_copy(
             src_ref=at, dst_ref=at,
-            send_sem=act_send.at[parity, c, which], recv_sem=act_recv.at[parity, c, which],
+            send_sem=act_send.at[parity, chunk_id(c)], recv_sem=act_recv.at[parity, chunk_id(c), which],
             device_id={"mp": flip(m, bit)}, device_id_type=MESH)
 
     def send(layer, parity, c):
@@ -394,8 +425,10 @@
                 act_copy(layer, parity, c, i).wait_recv()
 
     def sent(layer, parity, c):
-        for i in range(len(plan)):
-            act_copy(layer, parity, c, i).wait_send()
+        at = acts.at[layer, pl.ds(0, mp - 1), chunk(c)]
+        pltpu.make_async_remote_copy(
+            src_ref=at, dst_ref=at, send_sem=act_send.at[parity, chunk_id(c)], recv_sem=act_recv.at[parity, chunk_id(c), 0],
+            device_id={"mp": flip(m, 1)}, device_id_type=MESH).wait_send()
 
     def product(k, at):
         total = None
@@ -408,8 +441,11 @@
     last_up = (pieces - 1) * lane
     load.wait()
     with scope("s_begin"):
-        for c in order:
-            at = pl.ds(c * size, size)
+        for spot in range(len(order)):
+            c = (m % 2 if spot % 2 == 0 else 1 - m % 2), spot // 2
+            at = chunk(c)
+            if spot == 1:
+                sum1.done(pieces - 1)
             for index in range(mp):
                 before = partial[index, at] if pieces > 1 else states[index, at].astype(f32)
                 first = before + dot(full_b[pieces - 1, at], ups[index, last_up:last_up + lane, :])
@@ -419,20 +455,18 @@
             acts[1, m, at, :] = product(0, at).astype(bf16)
             send(1, 1, c)
         sum1.drain()
-        for j in range(pieces):
-            going[j][2]()
-            back[j][2]()
+        arrived(from_a.at[:, span], 0, 0).wait_send()
+        arrived(from_b.at[:, span], 1, 0).wait_send()
         for which in range(2):
-            for i in range(len(plan)):
-                early(which, i).wait_send()
+            early_sent(which)
     with scope("s_relay1"):
         relay(1, 1, order[0])
 
     def half_step(l, inside, first):
         k = 2 * l + inside
         for spot, c in enumerate(order):
-            at = pl.ds(c * size, size)
-            if spot + 1 < CHUNKS:
+            at = chunk(c)
+            if spot + 1 < len(order):
                 relay(k, inside, order[spot + 1])
             elif inside == 0:
                 relay(k + 1, 1, order[0])
@@ -471,30 +505,31 @@
     parts, part_lane = table.shape[0], table.shape[2]
     here = pl.ds(pl.multiple_of(g * ATOM_DEV, ATOM_DEV), ATOM_DEV)
     atom_span = pl.ds(0, atoms - ATOM_DEV)
-    gathers = [exchange(2 * pieces + p, piece(atoms_to, p, ATOM_DEV), piece(atoms_from, p, ATOM_DEV),
+    gathers = [exchange(2, 2 * pieces + p, piece(atoms_to, p, ATOM_DEV), piece(atoms_from, p, ATOM_DEV),
                         atoms_from.at[p, atom_span]) for p in range(parts)]
-    spreads = [exchange(2 * pieces + parts + p, lambda peer, p=p: piece(table, p, ATOM_DEV)(g),
+    spreads = [exchange(3, 2 * pieces + parts + p, lambda peer, p=p: piece(table, p, ATOM_DEV)(g),
                         piece(table, p, ATOM_DEV), table.at[p, atom_span]) for p in range(parts)]
 
     def columns(p):
         return slice(p * part_lane, (p + 1) * part_lane)
 
     with scope("s_collect"):
+        def collect(i, _):
+            at = pl.ds(pl.multiple_of(i * atom_rows, atom_rows), atom_rows)
+            ids = one_hot(atom_rows, atom_ref[...] - i * atom_rows)
+            high, low = halves(hidden[...])
+            total = dot(ids, high) + dot(ids, low)
+            for p in range(parts):
+                atoms_own[p, at] = total[:, columns(p)]
+                atoms_to[p, at] = total[:, columns(p)].astype(bf16)
+            return 0
+
+        lax.fori_loop(0, atoms // atom_rows, collect, 0)
         for p in range(parts):
-            def collect(i, _):
-                at = pl.ds(pl.multiple_of(i * atom_rows, atom_rows), atom_rows)
-                ids = one_hot(atom_rows, atom_ref[...] - i * atom_rows)
-                high, low = halves(hidden[:, columns(p)])
-                total = dot(ids, high) + dot(ids, low)
-                atoms_own[p, at] = total
-                atoms_to[p, at] = total.astype(bf16)
-                return 0
-
-            lax.fori_loop(0, atoms // atom_rows, collect, 0)
             gathers[p][0]()
     for p in range(parts):
         atoms_from[p, here] = jnp.zeros((ATOM_DEV, part_lane), bf16)
-    for c in range(CHUNKS):
+    for c in order:
         if layers > 1:
             sent(2 * layers - 2, 0, c)
         sent(2 * layers - 1, 1, c)
@@ -510,8 +545,7 @@
         table[p, here] = mine_out
         spreads[p][0]()
         atom_out_ref[:, columns(p)] = mine_out
-    for p in range(parts):
-        gathers[p][2]()
+    arrived(atoms_from.at[:, atom_span], 2, 0).wait_send()
     for p in range(parts):
         with scope("s_spreadwait%d" % p):
             spreads[p][1]()
@@ -522,8 +556,7 @@
 
         total = lax.fori_loop(0, atoms // atom_rows, spread, hidden[:, columns(p)])
         edge_out_ref[:, columns(p)] = total.astype(bf16)
-    for p in range(parts):
-        spreads[p][2]()
+    arrived(table.at[:, atom_span], 3, 0).wait_send()
 
 
 def hand_on(edge_ref, atom_ref, edge_out_ref, atom_out_ref, sem):
@@ -544,6 +577,7 @@
     maps = dense_weight.shape[0] * dense_weight.shape[1]
     tile = 2048 if slot_total <= 512 else 128
     atoms = graph * ATOM_DEV
+    chunks = 2 * len(chunks_of(rows // 2)[1])
     stages = mp.bit_length()
     extra = max(stages - 2, 1)
     half = rows // 2
@@ -571,12 +605,12 @@
     body = functools.partial(kernel, graph, mp, tile)
     before = [
         *inputs, dma((len(inputs) + 2,)),
-        vmem((mp, rows, width), bf16), vmem((mp, trip, width), bf16), dma((2, mp - 1)), dma((2, mp - 1)),
+        vmem((mp, rows, width), bf16), vmem((mp, trip, width), bf16), dma((2,)), dma((2, mp - 1)),
         vmem((maps,) + dense_weight.shape[2:], bf16), dma(()),
         *reduce_bufs, *reduce_bufs,
-        dma((2, pieces, stages)), dma((2, pieces, stages)),
+        dma((2, stages)), dma((2, pieces, stages)),
         *[vmem((pieces, slot_total, lane), bf16)] * 4,
-        dma((2 * pieces + 2 * parts,)), dma((2 * pieces + 2 * parts,)),
+        dma((4,)), dma((2 * pieces + 2 * parts,)),
         vmem((rows, slot_total), bf16), vmem((3 * pad, triplets), bf16), vmem((3 * pad, trip), bf16),
         vmem((trip, triplets), f32), vmem((slot_total, lane), f32),
     ]
@@ -594,7 +628,7 @@
         scratch_shapes=[
             *before, *hots,
             vmem((maps, mp, rows, width), bf16), vmem((mp, rows, width), f32), vmem((rows, width), f32),
-            dma((2, CHUNKS, mp - 1)), dma((2, CHUNKS, mp - 1)),
+            dma((2, chunks)), dma((2, chunks, mp - 1)),
             vmem(atom_buf, f32), vmem(atom_buf, bf16), vmem(atom_buf, bf16), vmem(atom_buf, bf16),
         ],
         compiler_params=pltpu.CompilerParams(

time: 99.4 us -> 97.5 us (0.981)
  Pallas kernels: 98.5 us -> 96.5 us
    pallas_call x1, Pallas kernels: 97.7 us -> 95.8 us  [local(): pl.pallas_call(body, out_shape=(pltpu.VMEM((rows, width), bf16), pltpu.VM...]
where the time goes in v3:
time: 97.5 us; the launch traced here: 97.3 us
  Pallas kernels  96.5 us (99%)
    pallas_call x1, Pallas kernels, local(): pl.pallas_call(body, out_shape=(pltpu.VMEM((rows, width), bf16), pltpu.VM...  95.8 us

profile of v3, /device:TPU:0, one launch (start us, length us, event | category | flops | bytes accessed | tf_op | source)
XLA Modules:
  0.0 97.3 jit_solution(9189390246772729194)
XLA Ops:
  0.6 95.8 %edge_block.1 = (bf16[512,384]{1,0:T(8,128)(2,1)S(1)}, bf16[32,384]{1,0:T(8,128)(2,1)S(1)}) custom-call(bf16[512,384]{1,0:T(8,128)(2,1)} %state_hbm.1, bf16[384,384]{1,0:T(8,128)(2,1)} %down_hbm.1, f32[42,4096]{1,0:T(8,128)} %basis_hbm.1, f32[42,384]{1,0:T(8,128)} %bw_hbm.1, bf16[384,384]{1,0:T(8,128)(2,1)} %up_hbm.1, bf16[6,1536,384]{2,1,0:T(8,128)(2,1)} %bitcast.5, ...), custom_call_target="tpu_custom_call" | custom-call | tf_op jit(solution)/shard_map/edge_block/pallas_call | solution.py:620
  96.4 0.8 hand_on.1

commit v4 on v3

--- a/solution.py
+++ b/solution.py
@@ -44,8 +44,7 @@
 
 
 def chunks_of(half):
-    quarter = half // 4
-    return (0, quarter, 3 * quarter), (quarter, 2 * quarter, quarter)
+    return (0, half // 2), (half // 2, half // 2)
 
 
 def gather_plan(mp):
@@ -63,7 +62,7 @@
     edge_out_ref, atom_out_ref,
     down_ref, basis_ref, bw_ref, lists_ref, in_ref, out_ref, live_ref, atom_ref, load_sem,
     states, ups, early_send, early_recv,
-    weight, weight_sem,
+    weight, weight_sem, opposite, feed_send, feed_y, feed_far, feed_near, core_send, core_recv,
     part_a, got_a, sum_a, more_a, full_a,
     part_b, got_b, sum_b, more_b, full_b,
     red_send, red_recv,
@@ -152,6 +151,60 @@
             if i not in relays_from:
                 early(which, i).wait_recv()
 
+    across_y = flip(m, mp // 2)
+    feeds = layers - 1
+    eighth = weight.shape[1] // 8
+    mine8 = g % 8
+
+    def xor(a, k):
+        for bit in (1, 2, 4):
+            if k & bit:
+                a = flip(a, bit)
+        return a
+
+    def part8(e):
+        return pl.ds(pl.multiple_of(e * eighth, eighth), eighth)
+
+    def feed_copy(src, f, e, sem, device):
+        return pltpu.make_async_remote_copy(
+            src_ref=src, dst_ref=opposite.at[f, part8(e)], send_sem=feed_send.at[f], recv_sem=sem,
+            device_id=device, device_id_type=MESH)
+
+    def enter(f):
+        return feed_copy(weight.at[2 * (f + 1), part8(mine8)], f, mine8, feed_y.at[f], {"mp": across_y})
+
+    def hop(f):
+        return feed_copy(opposite.at[f, part8(mine8)], f, mine8, feed_far.at[f], {"graph": xor(g, 4)})
+
+    def near(f, far):
+        e = xor(mine8, 4 * far)
+        return [feed_copy(opposite.at[f, part8(e)], f, e, feed_near.at[f, far], {"graph": xor(g, k)}) for k in (3, 2, 1)]
+
+    def feed_spread(f):
+        enter(f).wait_recv()
+        hop(f).start()
+        for copy in near(f, 0):
+            copy.start()
+
+    def feed_rest(f):
+        hop(f).wait_recv()
+        for copy in near(f, 1):
+            copy.start()
+
+    def feed_ready(f):
+        at = opposite.at[f, pl.ds(0, 3 * eighth)]
+        for far in range(2):
+            pltpu.make_async_remote_copy(
+                src_ref=at, dst_ref=at, send_sem=feed_send.at[f], recv_sem=feed_near.at[f, far],
+                device_id={"mp": across_y}, device_id_type=MESH).wait_recv()
+
+    def feed_sent():
+        for f in range(feeds):
+            at = opposite.at[f]
+            pltpu.make_async_remote_copy(
+                src_ref=at, dst_ref=at, send_sem=feed_send.at[f], recv_sem=feed_near.at[f, 0],
+                device_id={"mp": across_y}, device_id_type=MESH).wait_send()
+
     class Sum:
         def __init__(self, which, part, got, summed, more, full):
             self.which, self.part, self.got = which, part, got
@@ -277,9 +330,7 @@
         for j in range(pieces):
             sum0.across(j)
     up_in.wait()
-    for which in range(2):
-        for i in local[:1]:
-            early(which, i).start()
+    early(0, local[0]).start()
     out_in.wait()
     live_in.wait()
     if kept:
@@ -310,6 +361,10 @@
 
         tiles(angles)
 
+    load.wait()
+    if feeds:
+        enter(0).start()
+    early(1, local[0]).start()
     step_rows = min(slot_total, 512)
     own = pl.ds(pl.multiple_of(g * cap, cap), cap)
     span = pl.ds(0, slot_total - cap)
@@ -370,15 +425,19 @@
             back[j][1]()
         part_b[j] = dot(list_hot[...], from_b[j]).astype(bf16)
         sum1.into(j)
-        if j == 0:
-            with scope("s_early1"):
-                early_relay(1)
         if j + 1 < pieces:
             sum1.across(j)
     with scope("s_sum1"):
         for j in range(pieces - 2):
             sum1.home(j)
         sum1.across(pieces - 1)
+        with scope("s_early1"):
+            early_relay(1)
+        with scope("s_feedspread"):
+            if feeds:
+                feed_spread(0)
+            for f in range(1, feeds):
+                enter(f).start()
         early_finish(0)
         early_finish(1)
         if pieces > 1:
@@ -395,14 +454,14 @@
     def chunk(c):
         side, t = c
         start = side * half + starts[t]
-        return pl.ds(start if isinstance(side, int) else pl.multiple_of(start, half // 4), sizes[t])
+        return pl.ds(start if isinstance(side, int) else pl.multiple_of(start, half // 2), sizes[t])
 
     def chunk_id(c):
         return c[0] * len(sizes) + c[1]
 
     def act_copy(layer, parity, c, which):
         bit, off = plan[which]
-        at = acts.at[layer, other_of(off), chunk(c)]
+        at = acts.at[layer - 1, other_of(off), chunk(c)]
         return pltpu.make_async_remote_copy(
             src_ref=at, dst_ref=at,
             send_sem=act_send.at[parity, chunk_id(c)], recv_sem=act_recv.at[parity, chunk_id(c), which],
@@ -425,79 +484,129 @@
                 act_copy(layer, parity, c, i).wait_recv()
 
     def sent(layer, parity, c):
-        at = acts.at[layer, pl.ds(0, mp - 1), chunk(c)]
+        at = acts.at[layer - 1, pl.ds(0, mp - 1), chunk(c)]
         pltpu.make_async_remote_copy(
             src_ref=at, dst_ref=at, send_sem=act_send.at[parity, chunk_id(c)], recv_sem=act_recv.at[parity, chunk_id(c), 0],
             device_id={"mp": flip(m, 1)}, device_id_type=MESH).wait_send()
 
-    def product(k, at):
+    def product(k, at, held_weight):
         total = None
         for off in held:
             index = other_of(off)
-            term = dot(acts[k, index, at, :], weight[k, pl.ds(pl.multiple_of(index * width, width), width), :])
+            term = dot(acts[k - 1, index, at, :], held_weight[pl.ds(pl.multiple_of(index * width, width), width), :])
             total = term if total is None else total + term
         return silu(total)
 
+    def core_copy(layer, c, i):
+        at = acts.at[layer - 1, (m, across_y)[i], chunk(c)]
+        return pltpu.make_async_remote_copy(
+            src_ref=at, dst_ref=at, send_sem=core_send.at[chunk_id(c)], recv_sem=core_recv.at[chunk_id(c), i],
+            device_id={"mp": flip(m, 1)}, device_id_type=MESH)
+
+    def core_sent(layer, c):
+        at = acts.at[layer - 1, pl.ds(0, 2), chunk(c)]
+        pltpu.make_async_remote_copy(
+            src_ref=at, dst_ref=at, send_sem=core_send.at[chunk_id(c)], recv_sem=core_recv.at[chunk_id(c), 0],
+            device_id={"mp": flip(m, 1)}, device_id_type=MESH).wait_send()
+
     last_up = (pieces - 1) * lane
-    load.wait()
     with scope("s_begin"):
         for spot in range(len(order)):
             c = (m % 2 if spot % 2 == 0 else 1 - m % 2), spot // 2
             at = chunk(c)
             if spot == 1:
                 sum1.done(pieces - 1)
+            total = None
             for index in range(mp):
                 before = partial[index, at] if pieces > 1 else states[index, at].astype(f32)
                 first = before + dot(full_b[pieces - 1, at], ups[index, last_up:last_up + lane, :])
                 partial[index, at] = first
-                acts[0, index, at, :] = first.astype(bf16)
+                term = dot(first.astype(bf16), weight[0, index * width:(index + 1) * width, :])
+                total = term if total is None else total + term
             hidden[at, :] = partial[m, at]
-            acts[1, m, at, :] = product(0, at).astype(bf16)
-            send(1, 1, c)
+            acts[0, m, at, :] = silu(total).astype(bf16)
+            send(1, 0, c)
         sum1.drain()
         arrived(from_a.at[:, span], 0, 0).wait_send()
         arrived(from_b.at[:, span], 1, 0).wait_send()
         for which in range(2):
             early_sent(which)
-    with scope("s_relay1"):
-        relay(1, 1, order[0])
-
-    def half_step(l, inside, first):
-        k = 2 * l + inside
+    def update(k, c):
+        at = chunk(c)
+        value = (hidden[at, :] + product(k, at, weight.at[k])) * inv_root_two
+        hidden[at, :] = value
+        return value.astype(bf16)
+
+    with scope("s_layer0"):
+        relay(1, 0, order[0])
+        for spot, c in enumerate(order):
+            with scope("s_l0fin%d" % spot):
+                finish(1, 0, c)
+            value = update(1, c)
+            if layers > 1:
+                acts[1, m, chunk(c), :] = value
+                send(2, 1, c)
+            if spot + 1 < len(order):
+                with scope("s_l0rel%d" % spot):
+                    relay(1, 0, order[spot + 1])
+            if spot == 0:
+                with scope("s_feedrest0"):
+                    if feeds:
+                        feed_rest(0)
+                    for f in range(1, feeds):
+                        feed_spread(f)
+        with scope("s_feedrest1"):
+            for f in range(1, feeds):
+                feed_rest(f)
+        if layers > 1:
+            relay(2, 1, order[0])
+
+    def layer_step(l, _):
+        k, parity, f = 2 * l, l % 2, l - 1
+
+        def second(c):
+            for i in range(2):
+                core_copy(k + 1, c, i).wait_recv()
+            value = update(k + 1, c)
+
+            @pl.when(l + 1 < layers)
+            def _():
+                sent(k, 1 - parity, c)
+                acts[k + 1, m, chunk(c), :] = value
+                send(k + 2, 1 - parity, c)
+
+        with scope("s_feedwait"):
+            feed_ready(f)
         for spot, c in enumerate(order):
             at = chunk(c)
-            if spot + 1 < len(order):
-                relay(k, inside, order[spot + 1])
-            elif inside == 0:
-                relay(k + 1, 1, order[0])
-            elif not first or layers > 1:
-                @pl.when(l + 1 < layers)
-                def _():
-                    relay(k + 1, 0, order[0])
-            finish(k, inside, c)
-            value = product(k, at)
-            if inside == 0:
-                sent(k - 1, 1, c)
-                acts[k + 1, m, at, :] = value.astype(bf16)
-                send(k + 1, 1, c)
-            else:
-                value = (hidden[at, :] + value) * inv_root_two
-                hidden[at, :] = value
-
-                @pl.when(l + 1 < layers)
-                def _():
-                    if not first:
-                        sent(k - 1, 0, c)
-                    acts[k + 1, m, at, :] = value.astype(bf16)
-                    send(k + 1, 0, c)
-
-    def layer_step(l, _):
-        half_step(l, 0, False)
-        half_step(l, 1, False)
+            with scope("s_fin%d" % spot):
+                finish(k, parity, c)
+
+            @pl.when(l > 1)
+            def _():
+                core_sent(k - 1, c)
+
+            acts[k, m, at, :] = product(k, at, weight.at[k]).astype(bf16)
+            core_copy(k + 1, c, 0).start()
+            with scope("s_rel%d" % spot):
+                if spot + 1 < len(order):
+                    relay(k, parity, order[spot + 1])
+            acts[k, across_y, at, :] = product(k, at, opposite.at[f]).astype(bf16)
+            core_copy(k + 1, c, 1).start()
+            if spot >= 1:
+                with scope("s_second%d" % spot):
+                    second(order[spot - 1])
+
+        @pl.when(l + 1 < layers)
+        def _():
+            with scope("s_relnext"):
+                relay(k + 2, 1 - parity, order[0])
+
+        with scope("s_second_last"):
+            second(order[-1])
         return 0
 
     with scope("s_layers"):
-        half_step(0, 1, True)
         lax.fori_loop(1, layers, layer_step, 0)
 
     atom_in.wait()
@@ -530,9 +639,11 @@
     for p in range(parts):
         atoms_from[p, here] = jnp.zeros((ATOM_DEV, part_lane), bf16)
     for c in order:
+        sent(1, (layers - 1) % 2, c)
         if layers > 1:
-            sent(2 * layers - 2, 0, c)
-        sent(2 * layers - 1, 1, c)
+            sent(1, layers % 2, c)
+            core_sent(1, c)
+    feed_sent()
     for p in range(parts):
         with scope("s_atomwait%d" % p):
             gathers[p][1]()
@@ -577,6 +688,7 @@
     maps = dense_weight.shape[0] * dense_weight.shape[1]
     tile = 2048 if slot_total <= 512 else 128
     atoms = graph * ATOM_DEV
+    feeds = max(dense_weight.shape[0] - 1, 1)
     chunks = 2 * len(chunks_of(rows // 2)[1])
     stages = mp.bit_length()
     extra = max(stages - 2, 1)
@@ -607,6 +719,8 @@
         *inputs, dma((len(inputs) + 2,)),
         vmem((mp, rows, width), bf16), vmem((mp, trip, width), bf16), dma((2,)), dma((2, mp - 1)),
         vmem((maps,) + dense_weight.shape[2:], bf16), dma(()),
+        vmem((feeds,) + dense_weight.shape[2:], bf16), dma((feeds,)), dma((feeds,)), dma((feeds,)), dma((feeds, 2)),
+        dma((chunks,)), dma((chunks, 2)),
         *reduce_bufs, *reduce_bufs,
         dma((2, stages)), dma((2, pieces, stages)),
         *[vmem((pieces, slot_total, lane), bf16)] * 4,
@@ -627,7 +741,7 @@
         out_specs=(spec, spec),
         scratch_shapes=[
             *before, *hots,
-            vmem((maps, mp, rows, width), bf16), vmem((mp, rows, width), f32), vmem((rows, width), f32),
+            vmem((maps - 1, mp, rows, width), bf16), vmem((mp, rows, width), f32), vmem((rows, width), f32),
             dma((2, chunks)), dma((2, chunks, mp - 1)),
             vmem(atom_buf, f32), vmem(atom_buf, bf16), vmem(atom_buf, bf16), vmem(atom_buf, bf16),
         ],

time: 97.5 us -> 91.6 us (0.939)
  Pallas kernels: 96.5 us -> 90.7 us
    pallas_call x1, Pallas kernels: 95.8 us -> 89.9 us  [local(): pl.pallas_call(body, out_shape=(pltpu.VMEM((rows, width), bf16), pltpu.VM...]
where the time goes in v4:
time: 91.6 us; the launch traced here: 91.5 us
  Pallas kernels  90.7 us (99%)
    pallas_call x1, Pallas kernels, local(): pl.pallas_call(body, out_shape=(pltpu.VMEM((rows, width), bf16), pltpu.VM...  89.9 us

profile of v4, /device:TPU:0, one launch (start us, length us, event | category | flops | bytes accessed | tf_op | source)
XLA Modules:
  0.0 91.5 jit_solution(12882676191429822759)
XLA Ops:
  0.6 89.9 %edge_block.1 = (bf16[512,384]{1,0:T(8,128)(2,1)S(1)}, bf16[32,384]{1,0:T(8,128)(2,1)S(1)}) custom-call(bf16[512,384]{1,0:T(8,128)(2,1)} %state_hbm.1, bf16[384,384]{1,0:T(8,128)(2,1)} %down_hbm.1, f32[42,4096]{1,0:T(8,128)} %basis_hbm.1, f32[42,384]{1,0:T(8,128)} %bw_hbm.1, bf16[384,384]{1,0:T(8,128)(2,1)} %up_hbm.1, bf16[6,1536,384]{2,1,0:T(8,128)(2,1)} %bitcast.5, ...), custom_call_target="tpu_custom_call" | custom-call | tf_op jit(solution)/shard_map/edge_block/pallas_call | solution.py:734
  90.5 0.8 hand_on.1

commit v5 on v4

--- a/solution.py
+++ b/solution.py
@@ -61,8 +61,8 @@
     state_hbm, down_hbm, basis_hbm, bw_hbm, up_hbm, dense_hbm, lists_hbm, in_hbm, out_hbm, live_hbm, atom_hbm,
     edge_out_ref, atom_out_ref,
     down_ref, basis_ref, bw_ref, lists_ref, in_ref, out_ref, live_ref, atom_ref, load_sem,
-    states, ups, early_send, early_recv,
-    weight, weight_sem, opposite, feed_send, feed_y, feed_far, feed_near, core_send, core_recv,
+    states, ups, early_send, early_recv, up_send, up_recv,
+    weight, weight_sem, opposite, feed_send, feed_y, feed_far, near_recv, core_send, core_recv,
     part_a, got_a, sum_a, more_a, full_a,
     part_b, got_b, sum_b, more_b, full_b,
     red_send, red_recv,
@@ -126,6 +126,8 @@
     brings = {bit ^ off: i for i, (bit, off) in enumerate(plan)}
     relays_from = sorted({brings[plan[i][1]] for i in relayed})
 
+    across_y = flip(m, mp // 2)
+
     def early(which, i):
         bit, off = plan[i]
         at = (states, ups)[which].at[other_of(off)]
@@ -133,8 +135,26 @@
             src_ref=at, dst_ref=at, send_sem=early_send.at[which], recv_sem=early_recv.at[which, i],
             device_id={"mp": flip(m, bit)}, device_id_type=MESH)
 
+    trip_half = trip // 2
+    up_rows = pl.ds(pl.multiple_of((g % 2) * trip_half, trip_half), trip_half)
+
+    def up_copy(i):
+        at = ups.at[(m, across_y)[i], up_rows]
+        return pltpu.make_async_remote_copy(
+            src_ref=at, dst_ref=at, send_sem=up_send, recv_sem=up_recv.at[i],
+            device_id=({"mp": across_y}, {"graph": flip(g, 1)})[i], device_id_type=MESH)
+
+    def up_beside():
+        up_copy(0).wait_recv()
+        up_copy(1).start()
+
+    def up_home():
+        up_copy(1).wait_recv()
+        for i in relayed:
+            early(1, i).start()
+
     def early_sent(which):
-        at = (states, ups)[which].at[pl.ds(0, mp - 1)]
+        at = (states, ups)[which].at[pl.ds(0, mp - 1 - which)]
         pltpu.make_async_remote_copy(
             src_ref=at, dst_ref=at, send_sem=early_send.at[which], recv_sem=early_recv.at[which, 0],
             device_id={"mp": flip(m, 1)}, device_id_type=MESH).wait_send()
@@ -151,7 +171,6 @@
             if i not in relays_from:
                 early(which, i).wait_recv()
 
-    across_y = flip(m, mp // 2)
     feeds = layers - 1
     eighth = weight.shape[1] // 8
     mine8 = g % 8
@@ -170,39 +189,36 @@
             src_ref=src, dst_ref=opposite.at[f, part8(e)], send_sem=feed_send.at[f], recv_sem=sem,
             device_id=device, device_id_type=MESH)
 
-    def enter(f):
-        return feed_copy(weight.at[2 * (f + 1), part8(mine8)], f, mine8, feed_y.at[f], {"mp": across_y})
+    def enter(f, far):
+        e = xor(mine8, 4 * far)
+        return feed_copy(weight.at[2 * (f + 1), part8(e)], f, e, feed_y.at[f, far], {"mp": across_y})
 
     def hop(f):
         return feed_copy(opposite.at[f, part8(mine8)], f, mine8, feed_far.at[f], {"graph": xor(g, 4)})
 
-    def near(f, far):
+    def near(f, far, k):
         e = xor(mine8, 4 * far)
-        return [feed_copy(opposite.at[f, part8(e)], f, e, feed_near.at[f, far], {"graph": xor(g, k)}) for k in (3, 2, 1)]
-
-    def feed_spread(f):
-        enter(f).wait_recv()
-        hop(f).start()
-        for copy in near(f, 0):
-            copy.start()
-
-    def feed_rest(f):
-        hop(f).wait_recv()
-        for copy in near(f, 1):
-            copy.start()
+        return feed_copy(opposite.at[f, part8(e)], f, e, near_recv.at[f, far, k - 1], {"graph": xor(g, k)})
+
+    def corner(f, far):
+        came, goes = (2, 1) if far == 0 else (1, 2)
+        e = xor(mine8, 4 * far + came)
+        return feed_copy(opposite.at[f, part8(e)], f, e, near_recv.at[f, far, 2], {"graph": xor(g, goes)})
+
+    def feed_corner(f, far):
+        near(f, far, 2 if far == 0 else 1).wait_recv()
+        corner(f, far).start()
 
     def feed_ready(f):
-        at = opposite.at[f, pl.ds(0, 3 * eighth)]
         for far in range(2):
-            pltpu.make_async_remote_copy(
-                src_ref=at, dst_ref=at, send_sem=feed_send.at[f], recv_sem=feed_near.at[f, far],
-                device_id={"mp": across_y}, device_id_type=MESH).wait_recv()
+            near(f, far, 1 if far == 0 else 2).wait_recv()
+            corner(f, far).wait_recv()
 
     def feed_sent():
         for f in range(feeds):
             at = opposite.at[f]
             pltpu.make_async_remote_copy(
-                src_ref=at, dst_ref=at, send_sem=feed_send.at[f], recv_sem=feed_near.at[f, 0],
+                src_ref=at, dst_ref=at, send_sem=feed_send.at[f], recv_sem=near_recv.at[f, 0, 0],
                 device_id={"mp": across_y}, device_id_type=MESH).wait_send()
 
     class Sum:
@@ -363,8 +379,10 @@
 
     load.wait()
     if feeds:
-        enter(0).start()
-    early(1, local[0]).start()
+        enter(0, 0).start()
+    up_copy(0).start()
+    for f in range(1, feeds):
+        enter(f, 0).start()
     step_rows = min(slot_total, 512)
     own = pl.ds(pl.multiple_of(g * cap, cap), cap)
     span = pl.ds(0, slot_total - cap)
@@ -414,6 +432,8 @@
         from_b[j, own] = to_b[j, own]
     with scope("s_early0"):
         early_relay(0)
+    with scope("s_upbeside"):
+        up_beside()
 
     def add_up(j):
         for index in range(mp):
@@ -428,16 +448,17 @@
         if j + 1 < pieces:
             sum1.across(j)
     with scope("s_sum1"):
+        sum1.across(pieces - 1)
+        with scope("s_early1"):
+            up_home()
+        with scope("s_feedspread"):
+            if feeds:
+                enter(0, 0).wait_recv()
+                near(0, 0, 2).start()
+                near(0, 0, 1).start()
+                hop(0).start()
         for j in range(pieces - 2):
             sum1.home(j)
-        sum1.across(pieces - 1)
-        with scope("s_early1"):
-            early_relay(1)
-        with scope("s_feedspread"):
-            if feeds:
-                feed_spread(0)
-            for f in range(1, feeds):
-                enter(f).start()
         early_finish(0)
         early_finish(1)
         if pieces > 1:
@@ -516,6 +537,12 @@
             at = chunk(c)
             if spot == 1:
                 sum1.done(pieces - 1)
+            if spot == 3 and feeds:
+                with scope("s_corner00"):
+                    feed_corner(0, 0)
+                    for f in range(1, feeds):
+                        enter(f, 0).wait_recv()
+                        near(f, 0, 2).start()
             total = None
             for index in range(mp):
                 before = partial[index, at] if pieces > 1 else states[index, at].astype(f32)
@@ -531,6 +558,9 @@
         arrived(from_b.at[:, span], 1, 0).wait_send()
         for which in range(2):
             early_sent(which)
+        pltpu.make_async_remote_copy(
+            src_ref=ups.at[m], dst_ref=ups.at[m], send_sem=up_send, recv_sem=up_recv.at[0],
+            device_id={"mp": across_y}, device_id_type=MESH).wait_send()
     def update(k, c):
         at = chunk(c)
         value = (hidden[at, :] + product(k, at, weight.at[k])) * inv_root_two
@@ -538,28 +568,41 @@
         return value.astype(bf16)
 
     with scope("s_layer0"):
-        relay(1, 0, order[0])
+        with scope("s_feedrest0"):
+            for f in range(1, feeds):
+                enter(f, 1).start()
+            if feeds:
+                hop(0).wait_recv()
+                near(0, 1, 1).start()
+                near(0, 1, 2).start()
+        with scope("s_l0rel"):
+            relay(1, 0, order[0])
         for spot, c in enumerate(order):
             with scope("s_l0fin%d" % spot):
                 finish(1, 0, c)
+            with scope("s_l0rel%d" % spot):
+                if spot + 1 < len(order):
+                    relay(1, 0, order[spot + 1])
             value = update(1, c)
             if layers > 1:
                 acts[1, m, chunk(c), :] = value
                 send(2, 1, c)
-            if spot + 1 < len(order):
-                with scope("s_l0rel%d" % spot):
-                    relay(1, 0, order[spot + 1])
-            if spot == 0:
-                with scope("s_feedrest0"):
-                    if feeds:
-                        feed_rest(0)
+            with scope("s_l0feed%d" % spot):
+                if spot == 1 and feeds:
+                    feed_corner(0, 1)
                     for f in range(1, feeds):
-                        feed_spread(f)
+                        near(f, 0, 1).start()
+                if spot == 2:
+                    for f in range(1, feeds):
+                        feed_corner(f, 0)
+        if layers > 1:
+            with scope("s_l1rel"):
+                relay(2, 1, order[0])
         with scope("s_feedrest1"):
             for f in range(1, feeds):
-                feed_rest(f)
-        if layers > 1:
-            relay(2, 1, order[0])
+                enter(f, 1).wait_recv()
+                near(f, 1, 1).start()
+                near(f, 1, 2).start()
 
     def layer_step(l, _):
         k, parity, f = 2 * l, l % 2, l - 1
@@ -596,6 +639,12 @@
             if spot >= 1:
                 with scope("s_second%d" % spot):
                     second(order[spot - 1])
+            if spot == 1:
+                @pl.when(l == 1)
+                def _():
+                    with scope("s_corner11"):
+                        for later in range(1, feeds):
+                            feed_corner(later, 1)
 
         @pl.when(l + 1 < layers)
         def _():
@@ -717,9 +766,9 @@
     body = functools.partial(kernel, graph, mp, tile)
     before = [
         *inputs, dma((len(inputs) + 2,)),
-        vmem((mp, rows, width), bf16), vmem((mp, trip, width), bf16), dma((2,)), dma((2, mp - 1)),
+        vmem((mp, rows, width), bf16), vmem((mp, trip, width), bf16), dma((2,)), dma((2, mp - 1)), dma(()), dma((2,)),
         vmem((maps,) + dense_weight.shape[2:], bf16), dma(()),
-        vmem((feeds,) + dense_weight.shape[2:], bf16), dma((feeds,)), dma((feeds,)), dma((feeds,)), dma((feeds, 2)),
+        vmem((feeds,) + dense_weight.shape[2:], bf16), dma((feeds,)), dma((feeds, 2)), dma((feeds,)), dma((feeds, 2, 3)),
         dma((chunks,)), dma((chunks, 2)),
         *reduce_bufs, *reduce_bufs,
         dma((2, stages)), dma((2, pieces, stages)),

time: 91.6 us -> 88.6 us (0.967)
  Pallas kernels: 90.7 us -> 87.6 us
    pallas_call x1, Pallas kernels: 89.9 us -> 86.8 us  [local(): pl.pallas_call(body, out_shape=(pltpu.VMEM((rows, width), bf16), pltpu.VM...]
where the time goes in v5:
time: 88.6 us; the launch traced here: 88.4 us
  Pallas kernels  87.6 us (99%)
    pallas_call x1, Pallas kernels, local(): pl.pallas_call(body, out_shape=(pltpu.VMEM((rows, width), bf16), pltpu.VM...  86.8 us

profile of v5, /device:TPU:0, one launch (start us, length us, event | category | flops | bytes accessed | tf_op | source)
XLA Modules:
  0.0 88.4 jit_solution(14019425880313940085)
XLA Ops:
  0.6 86.8 %edge_block.1 = (bf16[512,384]{1,0:T(8,128)(2,1)S(1)}, bf16[32,384]{1,0:T(8,128)(2,1)S(1)}) custom-call(bf16[512,384]{1,0:T(8,128)(2,1)} %state_hbm.1, bf16[384,384]{1,0:T(8,128)(2,1)} %down_hbm.1, f32[42,4096]{1,0:T(8,128)} %basis_hbm.1, f32[42,384]{1,0:T(8,128)} %bw_hbm.1, bf16[384,384]{1,0:T(8,128)(2,1)} %up_hbm.1, bf16[6,1536,384]{2,1,0:T(8,128)(2,1)} %bitcast.5, ...), custom_call_target="tpu_custom_call" | custom-call | tf_op jit(solution)/shard_map/edge_block/pallas_call | solution.py:783
  87.5 0.8 hand_on.1

commit v6 on v5

--- a/solution.py
+++ b/solution.py
@@ -62,7 +62,7 @@
     edge_out_ref, atom_out_ref,
     down_ref, basis_ref, bw_ref, lists_ref, in_ref, out_ref, live_ref, atom_ref, load_sem,
     states, ups, early_send, early_recv, up_send, up_recv,
-    weight, weight_sem, opposite, feed_send, feed_y, feed_far, near_recv, core_send, core_recv,
+    weight, joint, weight_sem, feed_send, feed_y, feed_far, near_recv, core_send, core_recv,
     part_a, got_a, sum_a, more_a, full_a,
     part_b, got_b, sum_b, more_b, full_b,
     red_send, red_recv,
@@ -75,7 +75,7 @@
     m = lax.axis_index("mp")
     rows, width = hidden.shape
     trip = down_ref.shape[1]
-    layers = weight.shape[0] // 2
+    layers = weight.shape[0] - 1
     cap = lists_ref.shape[2]
     slot_total = graph * cap
     pieces, lane = to_a.shape[0], to_a.shape[2]
@@ -83,6 +83,7 @@
     triplets = in_ref.shape[1]
     atoms = graph * ATOM_DEV
     half = rows // 2
+    feeds = layers - 1
     bits = [1 << i for i in range(mp.bit_length() - 1)]
     stages = len(bits)
 
@@ -171,7 +172,6 @@
             if i not in relays_from:
                 early(which, i).wait_recv()
 
-    feeds = layers - 1
     eighth = weight.shape[1] // 8
     mine8 = g % 8
 
@@ -186,24 +186,24 @@
 
     def feed_copy(src, f, e, sem, device):
         return pltpu.make_async_remote_copy(
-            src_ref=src, dst_ref=opposite.at[f, part8(e)], send_sem=feed_send.at[f], recv_sem=sem,
+            src_ref=src, dst_ref=joint.at[f, part8(e), far_cols], send_sem=feed_send.at[f], recv_sem=sem,
             device_id=device, device_id_type=MESH)
 
     def enter(f, far):
         e = xor(mine8, 4 * far)
-        return feed_copy(weight.at[2 * (f + 1), part8(e)], f, e, feed_y.at[f, far], {"mp": across_y})
+        return feed_copy(joint.at[f, part8(e), own_cols], f, e, feed_y.at[f, far], {"mp": across_y})
 
     def hop(f):
-        return feed_copy(opposite.at[f, part8(mine8)], f, mine8, feed_far.at[f], {"graph": xor(g, 4)})
+        return feed_copy(joint.at[f, part8(mine8), far_cols], f, mine8, feed_far.at[f], {"graph": xor(g, 4)})
 
     def near(f, far, k):
         e = xor(mine8, 4 * far)
-        return feed_copy(opposite.at[f, part8(e)], f, e, near_recv.at[f, far, k - 1], {"graph": xor(g, k)})
+        return feed_copy(joint.at[f, part8(e), far_cols], f, e, near_recv.at[f, far, k - 1], {"graph": xor(g, k)})
 
     def corner(f, far):
         came, goes = (2, 1) if far == 0 else (1, 2)
         e = xor(mine8, 4 * far + came)
-        return feed_copy(opposite.at[f, part8(e)], f, e, near_recv.at[f, far, 2], {"graph": xor(g, goes)})
+        return feed_copy(joint.at[f, part8(e), far_cols], f, e, near_recv.at[f, far, 2], {"graph": xor(g, goes)})
 
     def feed_corner(f, far):
         near(f, far, 2 if far == 0 else 1).wait_recv()
@@ -216,7 +216,7 @@
 
     def feed_sent():
         for f in range(feeds):
-            at = opposite.at[f]
+            at = joint.at[f, :, far_cols]
             pltpu.make_async_remote_copy(
                 src_ref=at, dst_ref=at, send_sem=feed_send.at[f], recv_sem=near_recv.at[f, 0, 0],
                 device_id={"mp": across_y}, device_id_type=MESH).wait_send()
@@ -329,8 +329,12 @@
         pl.semaphore_wait(barrier, graph - 1 + len(bits))
     for j in range(pieces):
         sum0.into(j)
-    load = pltpu.make_async_copy(dense_hbm, weight, weight_sem)
-    load.start()
+    own_cols, far_cols = pl.ds(0, width), pl.ds(width, width)
+    places = [(0, weight.at[0])] + [(2 * l + 1, weight.at[1 + l]) for l in range(layers)]
+    places += [(2 * f + 2, joint.at[f, :, own_cols]) for f in range(feeds)]
+    loads_of_maps = [pltpu.make_async_copy(dense_hbm.at[k], at, weight_sem.at[k]) for k, at in places]
+    for load in loads_of_maps:
+        load.start()
 
     lists_in.wait()
     with scope("s_hots"):
@@ -377,7 +381,8 @@
 
         tiles(angles)
 
-    load.wait()
+    for load in loads_of_maps:
+        load.wait()
     if feeds:
         enter(0, 0).start()
     up_copy(0).start()
@@ -511,12 +516,8 @@
             device_id={"mp": flip(m, 1)}, device_id_type=MESH).wait_send()
 
     def product(k, at, held_weight):
-        total = None
-        for off in held:
-            index = other_of(off)
-            term = dot(acts[k - 1, index, at, :], held_weight[pl.ds(pl.multiple_of(index * width, width), width), :])
-            total = term if total is None else total + term
-        return silu(total)
+        rows_in = jnp.concatenate([acts[k - 1, index, at, :] for index in range(mp)], axis=1)
+        return silu(dot(rows_in, held_weight[...]))
 
     def core_copy(layer, c, i):
         at = acts.at[layer - 1, (m, across_y)[i], chunk(c)]
@@ -543,13 +544,13 @@
                     for f in range(1, feeds):
                         enter(f, 0).wait_recv()
                         near(f, 0, 2).start()
-            total = None
+            firsts = []
             for index in range(mp):
                 before = partial[index, at] if pieces > 1 else states[index, at].astype(f32)
                 first = before + dot(full_b[pieces - 1, at], ups[index, last_up:last_up + lane, :])
                 partial[index, at] = first
-                term = dot(first.astype(bf16), weight[0, index * width:(index + 1) * width, :])
-                total = term if total is None else total + term
+                firsts.append(first.astype(bf16))
+            total = dot(jnp.concatenate(firsts, axis=1), weight[0])
             hidden[at, :] = partial[m, at]
             acts[0, m, at, :] = silu(total).astype(bf16)
             send(1, 0, c)
@@ -561,9 +562,9 @@
         pltpu.make_async_remote_copy(
             src_ref=ups.at[m], dst_ref=ups.at[m], send_sem=up_send, recv_sem=up_recv.at[0],
             device_id={"mp": across_y}, device_id_type=MESH).wait_send()
-    def update(k, c):
+    def update(l, c):
         at = chunk(c)
-        value = (hidden[at, :] + product(k, at, weight.at[k])) * inv_root_two
+        value = (hidden[at, :] + product(2 * l + 1, at, weight.at[1 + l])) * inv_root_two
         hidden[at, :] = value
         return value.astype(bf16)
 
@@ -583,7 +584,7 @@
             with scope("s_l0rel%d" % spot):
                 if spot + 1 < len(order):
                     relay(1, 0, order[spot + 1])
-            value = update(1, c)
+            value = update(0, c)
             if layers > 1:
                 acts[1, m, chunk(c), :] = value
                 send(2, 1, c)
@@ -610,7 +611,7 @@
         def second(c):
             for i in range(2):
                 core_copy(k + 1, c, i).wait_recv()
-            value = update(k + 1, c)
+            value = update(l, c)
 
             @pl.when(l + 1 < layers)
             def _():
@@ -629,13 +630,14 @@
             def _():
                 core_sent(k - 1, c)
 
-            acts[k, m, at, :] = product(k, at, weight.at[k]).astype(bf16)
-            core_copy(k + 1, c, 0).start()
             with scope("s_rel%d" % spot):
                 if spot + 1 < len(order):
                     relay(k, parity, order[spot + 1])
-            acts[k, across_y, at, :] = product(k, at, opposite.at[f]).astype(bf16)
-            core_copy(k + 1, c, 1).start()
+            both = product(k, at, joint.at[f]).astype(bf16)
+            acts[k, m, at, :] = both[:, :width]
+            acts[k, across_y, at, :] = both[:, width:]
+            for i in range(2):
+                core_copy(k + 1, c, i).start()
             if spot >= 1:
                 with scope("s_second%d" % spot):
                     second(order[spot - 1])
@@ -737,7 +739,7 @@
     maps = dense_weight.shape[0] * dense_weight.shape[1]
     tile = 2048 if slot_total <= 512 else 128
     atoms = graph * ATOM_DEV
-    feeds = max(dense_weight.shape[0] - 1, 1)
+    feeds = dense_weight.shape[0] - 1
     chunks = 2 * len(chunks_of(rows // 2)[1])
     stages = mp.bit_length()
     extra = max(stages - 2, 1)
@@ -767,8 +769,8 @@
     before = [
         *inputs, dma((len(inputs) + 2,)),
         vmem((mp, rows, width), bf16), vmem((mp, trip, width), bf16), dma((2,)), dma((2, mp - 1)), dma(()), dma((2,)),
-        vmem((maps,) + dense_weight.shape[2:], bf16), dma(()),
-        vmem((feeds,) + dense_weight.shape[2:], bf16), dma((feeds,)), dma((feeds, 2)), dma((feeds,)), dma((feeds, 2, 3)),
+        vmem((dense_weight.shape[0] + 1,) + dense_weight.shape[2:], bf16),
+        vmem((feeds, dense_weight.shape[2], 2 * width), bf16), dma((maps,)), dma((feeds,)), dma((feeds, 2)), dma((feeds,)), dma((feeds, 2, 3)),
         dma((chunks,)), dma((chunks, 2)),
         *reduce_bufs, *reduce_bufs,
         dma((2, stages)), dma((2, pieces, stages)),

time: 88.6 us -> 87.1 us (0.983)
  Pallas kernels: 87.6 us -> 86.1 us
    pallas_call x1, Pallas kernels: 86.8 us -> 85.3 us  [local(): pl.pallas_call(body, out_shape=(pltpu.VMEM((rows, width), bf16), pltpu.VM...]
where the time goes in v6:
time: 87.1 us; the launch traced here: 86.9 us
  Pallas kernels  86.1 us (99%)
    pallas_call x1, Pallas kernels, local(): pl.pallas_call(body, out_shape=(pltpu.VMEM((rows, width), bf16), pltpu.VM...  85.3 us

profile of v6, /device:TPU:0, one launch (start us, length us, event | category | flops | bytes accessed | tf_op | source)
XLA Modules:
  0.0 86.9 jit_solution(11114429757939902363)
XLA Ops:
  0.6 85.3 %edge_block.1 = (bf16[512,384]{1,0:T(8,128)(2,1)S(1)}, bf16[32,384]{1,0:T(8,128)(2,1)S(1)}) custom-call(bf16[512,384]{1,0:T(8,128)(2,1)} %state_hbm.1, bf16[384,384]{1,0:T(8,128)(2,1)} %down_hbm.1, f32[42,4096]{1,0:T(8,128)} %basis_hbm.1, f32[42,384]{1,0:T(8,128)} %bw_hbm.1, bf16[384,384]{1,0:T(8,128)(2,1)} %up_hbm.1, bf16[6,1536,384]{2,1,0:T(8,128)(2,1)} %bitcast.5, ...), custom_call_target="tpu_custom_call" | custom-call | tf_op jit(solution)/shard_map/edge_block/pallas_call | solution.py:785
  86.0 0.8 hand_on.1

commit v7 on v6

--- a/solution.py
+++ b/solution.py
@@ -62,7 +62,7 @@
     edge_out_ref, atom_out_ref,
     down_ref, basis_ref, bw_ref, lists_ref, in_ref, out_ref, live_ref, atom_ref, load_sem,
     states, ups, early_send, early_recv, up_send, up_recv,
-    weight, joint, weight_sem, feed_send, feed_y, feed_far, near_recv, core_send, core_recv,
+    weight, joint, weight_sem, feed_send, feed_y, near_recv, core_send, core_recv,
     part_a, got_a, sum_a, more_a, full_a,
     part_b, got_b, sum_b, more_b, full_b,
     red_send, red_recv,
@@ -154,6 +154,13 @@
         for i in relayed:
             early(1, i).start()
 
+    def state_copy(i):
+        cut = rows // 8
+        at = states.at[m, (pl.ds(0, cut), pl.ds(cut, rows - cut))[i]]
+        return pltpu.make_async_remote_copy(
+            src_ref=at, dst_ref=at, send_sem=early_send.at[0], recv_sem=early_recv.at[0, local[0]],
+            device_id={"mp": across_y}, device_id_type=MESH)
+
     def early_sent(which):
         at = (states, ups)[which].at[pl.ds(0, mp - 1 - which)]
         pltpu.make_async_remote_copy(
@@ -192,9 +199,6 @@
     def enter(f, far):
         e = xor(mine8, 4 * far)
         return feed_copy(joint.at[f, part8(e), own_cols], f, e, feed_y.at[f, far], {"mp": across_y})
-
-    def hop(f):
-        return feed_copy(joint.at[f, part8(mine8), far_cols], f, mine8, feed_far.at[f], {"graph": xor(g, 4)})
 
     def near(f, far, k):
         e = xor(mine8, 4 * far)
@@ -329,6 +333,7 @@
         pl.semaphore_wait(barrier, graph - 1 + len(bits))
     for j in range(pieces):
         sum0.into(j)
+    state_copy(0).start()
     own_cols, far_cols = pl.ds(0, width), pl.ds(width, width)
     places = [(0, weight.at[0])] + [(2 * l + 1, weight.at[1 + l]) for l in range(layers)]
     places += [(2 * f + 2, joint.at[f, :, own_cols]) for f in range(feeds)]
@@ -350,7 +355,7 @@
         for j in range(pieces):
             sum0.across(j)
     up_in.wait()
-    early(0, local[0]).start()
+    state_copy(1).start()
     out_in.wait()
     live_in.wait()
     if kept:
@@ -386,6 +391,8 @@
     if feeds:
         enter(0, 0).start()
     up_copy(0).start()
+    if feeds:
+        enter(0, 1).start()
     for f in range(1, feeds):
         enter(f, 0).start()
     step_rows = min(slot_total, 512)
@@ -437,8 +444,6 @@
         from_b[j, own] = to_b[j, own]
     with scope("s_early0"):
         early_relay(0)
-    with scope("s_upbeside"):
-        up_beside()
 
     def add_up(j):
         for index in range(mp):
@@ -450,6 +455,9 @@
             back[j][1]()
         part_b[j] = dot(list_hot[...], from_b[j]).astype(bf16)
         sum1.into(j)
+        if j == 0:
+            with scope("s_upbeside"):
+                up_beside()
         if j + 1 < pieces:
             sum1.across(j)
     with scope("s_sum1"):
@@ -457,18 +465,20 @@
         with scope("s_early1"):
             up_home()
         with scope("s_feedspread"):
+            for f in range(1, feeds):
+                enter(f, 1).start()
             if feeds:
-                enter(0, 0).wait_recv()
-                near(0, 0, 2).start()
-                near(0, 0, 1).start()
-                hop(0).start()
+                for far in range(2):
+                    enter(0, far).wait_recv()
+                    near(0, far, 2 - far).start()
+                    near(0, far, 1 + far).start()
         for j in range(pieces - 2):
             sum1.home(j)
         early_finish(0)
         early_finish(1)
         if pieces > 1:
             sum1.home(pieces - 2)
-        for j in range(pieces - 1):
+        for j in range(pieces - 2):
             sum1.done(j)
             add_up(j)
         with scope("s_lasthome"):
@@ -531,29 +541,30 @@
             src_ref=at, dst_ref=at, send_sem=core_send.at[chunk_id(c)], recv_sem=core_recv.at[chunk_id(c), 0],
             device_id={"mp": flip(m, 1)}, device_id_type=MESH).wait_send()
 
-    last_up = (pieces - 1) * lane
+    late = range(max(pieces - 2, 0), pieces)
+    late_up = pl.ds(late[0] * lane, len(late) * lane)
     with scope("s_begin"):
         for spot in range(len(order)):
             c = (m % 2 if spot % 2 == 0 else 1 - m % 2), spot // 2
             at = chunk(c)
             if spot == 1:
-                sum1.done(pieces - 1)
-            if spot == 3 and feeds:
-                with scope("s_corner00"):
-                    feed_corner(0, 0)
-                    for f in range(1, feeds):
-                        enter(f, 0).wait_recv()
-                        near(f, 0, 2).start()
+                for j in late:
+                    sum1.done(j)
+            update_rows = jnp.concatenate([full_b[j, at] for j in late], axis=1)
             firsts = []
             for index in range(mp):
-                before = partial[index, at] if pieces > 1 else states[index, at].astype(f32)
-                first = before + dot(full_b[pieces - 1, at], ups[index, last_up:last_up + lane, :])
+                before = partial[index, at] if pieces > 2 else states[index, at].astype(f32)
+                first = before + dot(update_rows, ups[index, late_up, :])
                 partial[index, at] = first
                 firsts.append(first.astype(bf16))
             total = dot(jnp.concatenate(firsts, axis=1), weight[0])
             hidden[at, :] = partial[m, at]
             acts[0, m, at, :] = silu(total).astype(bf16)
             send(1, 0, c)
+        if feeds:
+            with scope("s_corner0"):
+                for far in range(2):
+                    feed_corner(0, far)
         sum1.drain()
         arrived(from_a.at[:, span], 0, 0).wait_send()
         arrived(from_b.at[:, span], 1, 0).wait_send()
@@ -571,11 +582,10 @@
     with scope("s_layer0"):
         with scope("s_feedrest0"):
             for f in range(1, feeds):
-                enter(f, 1).start()
-            if feeds:
-                hop(0).wait_recv()
-                near(0, 1, 1).start()
-                near(0, 1, 2).start()
+                for far in range(2):
+                    enter(f, far).wait_recv()
+                    near(f, far, 2 - far).start()
+                    near(f, far, 1 + far).start()
         with scope("s_l0rel"):
             relay(1, 0, order[0])
         for spot, c in enumerate(order):
@@ -589,22 +599,12 @@
                 acts[1, m, chunk(c), :] = value
                 send(2, 1, c)
             with scope("s_l0feed%d" % spot):
-                if spot == 1 and feeds:
-                    feed_corner(0, 1)
-                    for f in range(1, feeds):
-                        near(f, 0, 1).start()
                 if spot == 2:
                     for f in range(1, feeds):
                         feed_corner(f, 0)
         if layers > 1:
             with scope("s_l1rel"):
                 relay(2, 1, order[0])
-        with scope("s_feedrest1"):
-            for f in range(1, feeds):
-                enter(f, 1).wait_recv()
-                near(f, 1, 1).start()
-                near(f, 1, 2).start()
-
     def layer_step(l, _):
         k, parity, f = 2 * l, l % 2, l - 1
 
@@ -630,31 +630,32 @@
             def _():
                 core_sent(k - 1, c)
 
-            with scope("s_rel%d" % spot):
-                if spot + 1 < len(order):
-                    relay(k, parity, order[spot + 1])
             both = product(k, at, joint.at[f]).astype(bf16)
             acts[k, m, at, :] = both[:, :width]
             acts[k, across_y, at, :] = both[:, width:]
             for i in range(2):
                 core_copy(k + 1, c, i).start()
-            if spot >= 1:
-                with scope("s_second%d" % spot):
-                    second(order[spot - 1])
-            if spot == 1:
-                @pl.when(l == 1)
-                def _():
-                    with scope("s_corner11"):
+            last = spot + 1 == len(order)
+            with scope("s_rel%d" % spot):
+                if not last:
+                    relay(k, parity, order[spot + 1])
+            with scope("s_second%d" % spot):
+                if spot == 0:
+                    second(c)
+
+                    @pl.when(l == 1)
+                    def _():
                         for later in range(1, feeds):
                             feed_corner(later, 1)
-
-        @pl.when(l + 1 < layers)
-        def _():
-            with scope("s_relnext"):
-                relay(k + 2, 1 - parity, order[0])
-
-        with scope("s_second_last"):
-            second(order[-1])
+                elif spot > 1:
+                    second(order[spot - 1])
+            if last:
+                with scope("s_relnext"):
+                    @pl.when(l + 1 < layers)
+                    def _():
+                        relay(k + 2, 1 - parity, order[0])
+                with scope("s_last"):
+                    second(c)
         return 0
 
     with scope("s_layers"):
@@ -770,7 +771,7 @@
         *inputs, dma((len(inputs) + 2,)),
         vmem((mp, rows, width), bf16), vmem((mp, trip, width), bf16), dma((2,)), dma((2, mp - 1)), dma(()), dma((2,)),
         vmem((dense_weight.shape[0] + 1,) + dense_weight.shape[2:], bf16),
-        vmem((feeds, dense_weight.shape[2], 2 * width), bf16), dma((maps,)), dma((feeds,)), dma((feeds, 2)), dma((feeds,)), dma((feeds, 2, 3)),
+        vmem((feeds, dense_weight.shape[2], 2 * width), bf16), dma((maps,)), dma((feeds,)), dma((feeds, 2)), dma((feeds, 2, 3)),
         dma((chunks,)), dma((chunks, 2)),
         *reduce_bufs, *reduce_bufs,
         dma((2, stages)), dma((2, pieces, stages)),

time: 87.1 us -> 85 us (0.976)
  Pallas kernels: 86.1 us -> 84 us
    pallas_call x1, Pallas kernels: 85.3 us -> 83.3 us  [local(): pl.pallas_call(body, out_shape=(pltpu.VMEM((rows, width), bf16), pltpu.VM...]
where the time goes in v7:
time: 85 us; the launch traced here: 84.8 us
  Pallas kernels  84 us (99%)
    pallas_call x1, Pallas kernels, local(): pl.pallas_call(body, out_shape=(pltpu.VMEM((rows, width), bf16), pltpu.VM...  83.3 us

profile of v7, /device:TPU:0, one launch (start us, length us, event | category | flops | bytes accessed | tf_op | source)
XLA Modules:
  0.0 84.8 jit_solution(4924793021215710231)
XLA Ops:
  0.6 83.3 %edge_block.1 = (bf16[512,384]{1,0:T(8,128)(2,1)S(1)}, bf16[32,384]{1,0:T(8,128)(2,1)S(1)}) custom-call(bf16[512,384]{1,0:T(8,128)(2,1)} %state_hbm.1, bf16[384,384]{1,0:T(8,128)(2,1)} %down_hbm.1, f32[42,4096]{1,0:T(8,128)} %basis_hbm.1, f32[42,384]{1,0:T(8,128)} %bw_hbm.1, bf16[384,384]{1,0:T(8,128)(2,1)} %up_hbm.1, bf16[6,1536,384]{2,1,0:T(8,128)(2,1)} %bitcast.5, ...), custom_call_target="tpu_custom_call" | custom-call | tf_op jit(solution)/shard_map/edge_block/pallas_call | solution.py:786
  83.9 0.8 hand_on.1

commit v8 on v7

--- a/solution.py
+++ b/solution.py
@@ -133,7 +133,7 @@
         bit, off = plan[i]
         at = (states, ups)[which].at[other_of(off)]
         return pltpu.make_async_remote_copy(
-            src_ref=at, dst_ref=at, send_sem=early_send.at[which], recv_sem=early_recv.at[which, i],
+            src_ref=at, dst_ref=at, send_sem=early_send.at[which], recv_sem=early_recv.at[which, 0 if i in relays_from else 1],
             device_id={"mp": flip(m, bit)}, device_id_type=MESH)
 
     trip_half = trip // 2
@@ -158,7 +158,7 @@
         cut = rows // 8
         at = states.at[m, (pl.ds(0, cut), pl.ds(cut, rows - cut))[i]]
         return pltpu.make_async_remote_copy(
-            src_ref=at, dst_ref=at, send_sem=early_send.at[0], recv_sem=early_recv.at[0, local[0]],
+            src_ref=at, dst_ref=at, send_sem=early_send.at[0], recv_sem=early_recv.at[0, 0],
             device_id={"mp": across_y}, device_id_type=MESH)
 
     def early_sent(which):
@@ -175,9 +175,10 @@
             early(which, i).start()
 
     def early_finish(which):
-        for i in range(len(plan)):
-            if i not in relays_from:
-                early(which, i).wait_recv()
+        at = (states, ups)[which].at[pl.ds(0, len(plan) - len(relays_from))]
+        pltpu.make_async_remote_copy(
+            src_ref=at, dst_ref=at, send_sem=early_send.at[which], recv_sem=early_recv.at[which, 1],
+            device_id={"mp": flip(m, 1)}, device_id_type=MESH).wait_recv()
 
     eighth = weight.shape[1] // 8
     mine8 = g % 8
@@ -202,21 +203,23 @@
 
     def near(f, far, k):
         e = xor(mine8, 4 * far)
-        return feed_copy(joint.at[f, part8(e), far_cols], f, e, near_recv.at[f, far, k - 1], {"graph": xor(g, k)})
+        return feed_copy(joint.at[f, part8(e), far_cols], f, e, near_recv.at[f, far, 0 if k == 2 - far else 1], {"graph": xor(g, k)})
 
     def corner(f, far):
         came, goes = (2, 1) if far == 0 else (1, 2)
         e = xor(mine8, 4 * far + came)
-        return feed_copy(joint.at[f, part8(e), far_cols], f, e, near_recv.at[f, far, 2], {"graph": xor(g, goes)})
+        return feed_copy(joint.at[f, part8(e), far_cols], f, e, near_recv.at[f, far, 1], {"graph": xor(g, goes)})
 
     def feed_corner(f, far):
         near(f, far, 2 if far == 0 else 1).wait_recv()
         corner(f, far).start()
 
     def feed_ready(f):
+        at = joint.at[f, pl.ds(0, 2 * eighth), far_cols]
         for far in range(2):
-            near(f, far, 1 if far == 0 else 2).wait_recv()
-            corner(f, far).wait_recv()
+            pltpu.make_async_remote_copy(
+                src_ref=at, dst_ref=at, send_sem=feed_send.at[f], recv_sem=near_recv.at[f, far, 1],
+                device_id={"mp": across_y}, device_id_type=MESH).wait_recv()
 
     def feed_sent():
         for f in range(feeds):
@@ -337,9 +340,8 @@
     own_cols, far_cols = pl.ds(0, width), pl.ds(width, width)
     places = [(0, weight.at[0])] + [(2 * l + 1, weight.at[1 + l]) for l in range(layers)]
     places += [(2 * f + 2, joint.at[f, :, own_cols]) for f in range(feeds)]
-    loads_of_maps = [pltpu.make_async_copy(dense_hbm.at[k], at, weight_sem.at[k]) for k, at in places]
-    for load in loads_of_maps:
-        load.start()
+    for k, at in places:
+        pltpu.make_async_copy(dense_hbm.at[k], at, weight_sem.at[1 if k and k % 2 == 0 else 0]).start()
 
     lists_in.wait()
     with scope("s_hots"):
@@ -386,8 +388,9 @@
 
         tiles(angles)
 
-    for load in loads_of_maps:
-        load.wait()
+    pltpu.make_async_copy(weight, weight, weight_sem.at[0]).wait()
+    if feeds:
+        pltpu.make_async_copy(joint.at[:, :, own_cols], joint.at[:, :, own_cols], weight_sem.at[1]).wait()
     if feeds:
         enter(0, 0).start()
     up_copy(0).start()
@@ -500,7 +503,7 @@
         at = acts.at[layer - 1, other_of(off), chunk(c)]
         return pltpu.make_async_remote_copy(
             src_ref=at, dst_ref=at,
-            send_sem=act_send.at[parity, chunk_id(c)], recv_sem=act_recv.at[parity, chunk_id(c), which],
+            send_sem=act_send.at[parity, chunk_id(c)], recv_sem=act_recv.at[parity, chunk_id(c), 0 if which in relays_from else 1],
             device_id={"mp": flip(m, bit)}, device_id_type=MESH)
 
     def send(layer, parity, c):
@@ -515,9 +518,11 @@
             act_copy(layer, parity, c, i).start()
 
     def finish(layer, parity, c):
-        for i in range(len(plan)):
-            if i not in relays_from:
-                act_copy(layer, parity, c, i).wait_recv()
+        at = acts.at[layer - 1, pl.ds(0, len(plan) - len(relays_from)), chunk(c)]
+        pltpu.make_async_remote_copy(
+            src_ref=at, dst_ref=at, send_sem=act_send.at[parity, chunk_id(c)],
+            recv_sem=act_recv.at[parity, chunk_id(c), 1],
+            device_id={"mp": flip(m, 1)}, device_id_type=MESH).wait_recv()
 
     def sent(layer, parity, c):
         at = acts.at[layer - 1, pl.ds(0, mp - 1), chunk(c)]
@@ -532,14 +537,17 @@
     def core_copy(layer, c, i):
         at = acts.at[layer - 1, (m, across_y)[i], chunk(c)]
         return pltpu.make_async_remote_copy(
-            src_ref=at, dst_ref=at, send_sem=core_send.at[chunk_id(c)], recv_sem=core_recv.at[chunk_id(c), i],
+            src_ref=at, dst_ref=at, send_sem=core_send.at[chunk_id(c)], recv_sem=core_recv.at[chunk_id(c)],
             device_id={"mp": flip(m, 1)}, device_id_type=MESH)
 
+    def core_both(layer, c):
+        at = acts.at[layer - 1, pl.ds(0, 2), chunk(c)]
+        return pltpu.make_async_remote_copy(
+            src_ref=at, dst_ref=at, send_sem=core_send.at[chunk_id(c)], recv_sem=core_recv.at[chunk_id(c)],
+            device_id={"mp": flip(m, 1)}, device_id_type=MESH)
+
     def core_sent(layer, c):
-        at = acts.at[layer - 1, pl.ds(0, 2), chunk(c)]
-        pltpu.make_async_remote_copy(
-            src_ref=at, dst_ref=at, send_sem=core_send.at[chunk_id(c)], recv_sem=core_recv.at[chunk_id(c), 0],
-            device_id={"mp": flip(m, 1)}, device_id_type=MESH).wait_send()
+        core_both(layer, c).wait_send()
 
     late = range(max(pieces - 2, 0), pieces)
     late_up = pl.ds(late[0] * lane, len(late) * lane)
@@ -573,6 +581,32 @@
         pltpu.make_async_remote_copy(
             src_ref=ups.at[m], dst_ref=ups.at[m], send_sem=up_send, recv_sem=up_recv.at[0],
             device_id={"mp": across_y}, device_id_type=MESH).wait_send()
+    atom_in.wait()
+    atom_rows = min(atoms, 256)
+    parts, part_lane = table.shape[0], table.shape[2]
+
+    def columns(p):
+        return slice(p * part_lane, (p + 1) * part_lane)
+
+    def collect(c):
+        at = chunk(c)
+        stacked = jnp.concatenate(halves(hidden[at, :]), axis=0)
+
+        def one(i, _):
+            here_rows = pl.ds(pl.multiple_of(i * atom_rows, atom_rows), atom_rows)
+            ids = one_hot(atom_rows, atom_ref[:, at] - i * atom_rows)
+            total = dot(jnp.concatenate([ids, ids], axis=1), stacked)
+            for p in range(parts):
+                sums = total[:, columns(p)]
+                if c != order[0]:
+                    sums += atoms_own[p, here_rows]
+                atoms_own[p, here_rows] = sums
+                if c == order[-1]:
+                    atoms_to[p, here_rows] = sums.astype(bf16)
+            return 0
+
+        lax.fori_loop(0, atoms // atom_rows, one, 0)
+
     def update(l, c):
         at = chunk(c)
         value = (hidden[at, :] + product(2 * l + 1, at, weight.at[1 + l])) * inv_root_two
@@ -609,8 +643,7 @@
         k, parity, f = 2 * l, l % 2, l - 1
 
         def second(c):
-            for i in range(2):
-                core_copy(k + 1, c, i).wait_recv()
+            core_both(k + 1, c).wait_recv()
             value = update(l, c)
 
             @pl.when(l + 1 < layers)
@@ -619,12 +652,14 @@
                 acts[k + 1, m, chunk(c), :] = value
                 send(k + 2, 1 - parity, c)
 
+            @pl.when(l + 1 == layers)
+            def _():
+                collect(c)
+
         with scope("s_feedwait"):
             feed_ready(f)
-        for spot, c in enumerate(order):
+        def opening(c):
             at = chunk(c)
-            with scope("s_fin%d" % spot):
-                finish(k, parity, c)
 
             @pl.when(l > 1)
             def _():
@@ -635,35 +670,38 @@
             acts[k, across_y, at, :] = both[:, width:]
             for i in range(2):
                 core_copy(k + 1, c, i).start()
-            last = spot + 1 == len(order)
-            with scope("s_rel%d" % spot):
-                if not last:
-                    relay(k, parity, order[spot + 1])
-            with scope("s_second%d" % spot):
-                if spot == 0:
-                    second(c)
+
+        for spot in range(0, len(order), 2):
+            one, two = order[spot:spot + 2]
+            with scope("s_finA%d" % spot):
+                finish(k, parity, one)
+            with scope("s_relA%d" % spot):
+                relay(k, parity, two)
+            opening(one)
+            with scope("s_finB%d" % spot):
+                finish(k, parity, two)
+            opening(two)
+            with scope("s_secA%d" % spot):
+                second(one)
+            with scope("s_relB%d" % spot):
+                if spot + 2 < len(order):
+                    relay(k, parity, order[spot + 2])
 
                     @pl.when(l == 1)
                     def _():
                         for later in range(1, feeds):
                             feed_corner(later, 1)
-                elif spot > 1:
-                    second(order[spot - 1])
-            if last:
-                with scope("s_relnext"):
+                else:
                     @pl.when(l + 1 < layers)
                     def _():
                         relay(k + 2, 1 - parity, order[0])
-                with scope("s_last"):
-                    second(c)
+            with scope("s_secB%d" % spot):
+                second(two)
         return 0
 
     with scope("s_layers"):
         lax.fori_loop(1, layers, layer_step, 0)
 
-    atom_in.wait()
-    atom_rows = min(atoms, 256)
-    parts, part_lane = table.shape[0], table.shape[2]
     here = pl.ds(pl.multiple_of(g * ATOM_DEV, ATOM_DEV), ATOM_DEV)
     atom_span = pl.ds(0, atoms - ATOM_DEV)
     gathers = [exchange(2, 2 * pieces + p, piece(atoms_to, p, ATOM_DEV), piece(atoms_from, p, ATOM_DEV),
@@ -671,23 +709,11 @@
     spreads = [exchange(3, 2 * pieces + parts + p, lambda peer, p=p: piece(table, p, ATOM_DEV)(g),
                         piece(table, p, ATOM_DEV), table.at[p, atom_span]) for p in range(parts)]
 
-    def columns(p):
-        return slice(p * part_lane, (p + 1) * part_lane)
-
-    with scope("s_collect"):
-        def collect(i, _):
-            at = pl.ds(pl.multiple_of(i * atom_rows, atom_rows), atom_rows)
-            ids = one_hot(atom_rows, atom_ref[...] - i * atom_rows)
-            high, low = halves(hidden[...])
-            total = dot(ids, high) + dot(ids, low)
-            for p in range(parts):
-                atoms_own[p, at] = total[:, columns(p)]
-                atoms_to[p, at] = total[:, columns(p)].astype(bf16)
-            return 0
-
-        lax.fori_loop(0, atoms // atom_rows, collect, 0)
-        for p in range(parts):
-            gathers[p][0]()
+    if layers == 1:
+        for c in order:
+            collect(c)
+    for p in range(parts):
+        gathers[p][0]()
     for p in range(parts):
         atoms_from[p, here] = jnp.zeros((ATOM_DEV, part_lane), bf16)
     for c in order:
@@ -769,10 +795,10 @@
     body = functools.partial(kernel, graph, mp, tile)
     before = [
         *inputs, dma((len(inputs) + 2,)),
-        vmem((mp, rows, width), bf16), vmem((mp, trip, width), bf16), dma((2,)), dma((2, mp - 1)), dma(()), dma((2,)),
+        vmem((mp, rows, width), bf16), vmem((mp, trip, width), bf16), dma((2,)), dma((2, 2)), dma(()), dma((2,)),
         vmem((dense_weight.shape[0] + 1,) + dense_weight.shape[2:], bf16),
-        vmem((feeds, dense_weight.shape[2], 2 * width), bf16), dma((maps,)), dma((feeds,)), dma((feeds, 2)), dma((feeds, 2, 3)),
-        dma((chunks,)), dma((chunks, 2)),
+        vmem((feeds, dense_weight.shape[2], 2 * width), bf16), dma((2,)), dma((feeds,)), dma((feeds, 2)), dma((feeds, 2, 2)),
+        dma((chunks,)), dma((chunks,)),
         *reduce_bufs, *reduce_bufs,
         dma((2, stages)), dma((2, pieces, stages)),
         *[vmem((pieces, slot_total, lane), bf16)] * 4,
@@ -794,7 +820,7 @@
         scratch_shapes=[
             *before, *hots,
             vmem((maps - 1, mp, rows, width), bf16), vmem((mp, rows, width), f32), vmem((rows, width), f32),
-            dma((2, chunks)), dma((2, chunks, mp - 1)),
+            dma((2, chunks)), dma((2, chunks, 2)),
             vmem(atom_buf, f32), vmem(atom_buf, bf16), vmem(atom_buf, bf16), vmem(atom_buf, bf16),
         ],
         compiler_params=pltpu.CompilerParams(

time: 85 us -> 84.5 us (level)
  no operation moved by 1% of the time
where the time goes in v8:
time: 84.5 us; the launch traced here: 84.4 us
  Pallas kernels  83.6 us (99%)
    pallas_call x1, Pallas kernels, local(): pl.pallas_call(body, out_shape=(pltpu.VMEM((rows, width), bf16), pltpu.VM...  82.8 us

profile of v8, /device:TPU:0, one launch (start us, length us, event | category | flops | bytes accessed | tf_op | source)
XLA Modules:
  0.0 84.4 jit_solution(13107169333520923302)
XLA Ops:
  0.6 82.8 %edge_block.1 = (bf16[512,384]{1,0:T(8,128)(2,1)S(1)}, bf16[32,384]{1,0:T(8,128)(2,1)S(1)}) custom-call(bf16[512,384]{1,0:T(8,128)(2,1)} %state_hbm.1, bf16[384,384]{1,0:T(8,128)(2,1)} %down_hbm.1, f32[42,4096]{1,0:T(8,128)} %basis_hbm.1, f32[42,384]{1,0:T(8,128)} %bw_hbm.1, bf16[384,384]{1,0:T(8,128)(2,1)} %up_hbm.1, bf16[6,1536,384]{2,1,0:T(8,128)(2,1)} %bitcast.5, ...), custom_call_target="tpu_custom_call" | custom-call | tf_op jit(solution)/shard_map/edge_block/pallas_call | solution.py:812
  83.5 0.8 hand_on.1

commit v9 on v8

--- a/solution.py
+++ b/solution.py
@@ -401,8 +401,9 @@
     step_rows = min(slot_total, 512)
     own = pl.ds(pl.multiple_of(g * cap, cap), cap)
     span = pl.ds(0, slot_total - cap)
+    most = xc_recv.shape[0] // 2
     going = [exchange(0, j, piece(to_a, j, cap), piece(from_a, j, cap), from_a.at[j, span]) for j in range(pieces)]
-    back = [exchange(1, pieces + j, piece(to_b, j, cap), piece(from_b, j, cap), from_b.at[j, span])
+    back = [exchange(1, most + j, piece(to_b, j, cap), piece(from_b, j, cap), from_b.at[j, span])
             for j in range(pieces)]
 
     def pick_piece(j):
@@ -417,12 +418,9 @@
         from_a[j, own] = to_a[j, own]
 
     with scope("s_home"):
-        sum0.home(0)
-    with scope("s_home1"):
-        for j in range(1, pieces):
+        for j in range(pieces):
             sum0.home(j)
-            pick_piece(j - 1)
-        pick_piece(pieces - 1)
+            pick_piece(j)
     for which in range(2):
         for i in local[1:]:
             early(which, i).start()
@@ -628,6 +626,9 @@
             with scope("s_l0rel%d" % spot):
                 if spot + 1 < len(order):
                     relay(1, 0, order[spot + 1])
+            if spot + 1 == len(order) and layers > 1:
+                with scope("s_l1rel"):
+                    relay(2, 1, order[0])
             value = update(0, c)
             if layers > 1:
                 acts[1, m, chunk(c), :] = value
@@ -636,9 +637,7 @@
                 if spot == 2:
                     for f in range(1, feeds):
                         feed_corner(f, 0)
-        if layers > 1:
-            with scope("s_l1rel"):
-                relay(2, 1, order[0])
+
     def layer_step(l, _):
         k, parity, f = 2 * l, l % 2, l - 1
 
@@ -704,9 +703,9 @@
 
     here = pl.ds(pl.multiple_of(g * ATOM_DEV, ATOM_DEV), ATOM_DEV)
     atom_span = pl.ds(0, atoms - ATOM_DEV)
-    gathers = [exchange(2, 2 * pieces + p, piece(atoms_to, p, ATOM_DEV), piece(atoms_from, p, ATOM_DEV),
+    gathers = [exchange(0, p, piece(atoms_to, p, ATOM_DEV), piece(atoms_from, p, ATOM_DEV),
                         atoms_from.at[p, atom_span]) for p in range(parts)]
-    spreads = [exchange(3, 2 * pieces + parts + p, lambda peer, p=p: piece(table, p, ATOM_DEV)(g),
+    spreads = [exchange(1, most + p, lambda peer, p=p: piece(table, p, ATOM_DEV)(g),
                         piece(table, p, ATOM_DEV), table.at[p, atom_span]) for p in range(parts)]
 
     if layers == 1:
@@ -734,7 +733,7 @@
         table[p, here] = mine_out
         spreads[p][0]()
         atom_out_ref[:, columns(p)] = mine_out
-    arrived(atoms_from.at[:, atom_span], 2, 0).wait_send()
+    arrived(atoms_from.at[:, atom_span], 0, 0).wait_send()
     for p in range(parts):
         with scope("s_spreadwait%d" % p):
             spreads[p][1]()
@@ -745,7 +744,7 @@
 
         total = lax.fori_loop(0, atoms // atom_rows, spread, hidden[:, columns(p)])
         edge_out_ref[:, columns(p)] = total.astype(bf16)
-    arrived(table.at[:, atom_span], 3, 0).wait_send()
+    arrived(table.at[:, atom_span], 1, 0).wait_send()
 
 
 def hand_on(edge_ref, atom_ref, edge_out_ref, atom_out_ref, sem):
@@ -802,7 +801,7 @@
         *reduce_bufs, *reduce_bufs,
         dma((2, stages)), dma((2, pieces, stages)),
         *[vmem((pieces, slot_total, lane), bf16)] * 4,
-        dma((4,)), dma((2 * pieces + 2 * parts,)),
+        dma((2,)), dma((2 * max(pieces, parts),)),
         vmem((rows, slot_total), bf16), vmem((3 * pad, triplets), bf16), vmem((3 * pad, trip), bf16),
         vmem((trip, triplets), f32), vmem((slot_total, lane), f32),
     ]

time: 84.5 us -> 84.2 us (level)
  no operation moved by 1% of the time
where the time goes in v9:
time: 84.2 us; the launch traced here: 84.1 us
  Pallas kernels  83.3 us (99%)
    pallas_call x1, Pallas kernels, local(): pl.pallas_call(body, out_shape=(pltpu.VMEM((rows, width), bf16), pltpu.VM...  82.5 us

profile of v9, /device:TPU:0, one launch (start us, length us, event | category | flops | bytes accessed | tf_op | source)
XLA Modules:
  0.0 84.1 jit_solution(11719820802494267638)
XLA Ops:
  0.6 82.5 %edge_block.1 = (bf16[512,384]{1,0:T(8,128)(2,1)S(1)}, bf16[32,384]{1,0:T(8,128)(2,1)S(1)}) custom-call(bf16[512,384]{1,0:T(8,128)(2,1)} %state_hbm.1, bf16[384,384]{1,0:T(8,128)(2,1)} %down_hbm.1, f32[42,4096]{1,0:T(8,128)} %basis_hbm.1, f32[42,384]{1,0:T(8,128)} %bw_hbm.1, bf16[384,384]{1,0:T(8,128)(2,1)} %up_hbm.1, bf16[6,1536,384]{2,1,0:T(8,128)(2,1)} %bitcast.5, ...), custom_call_target="tpu_custom_call" | custom-call | tf_op jit(solution)/shard_map/edge_block/pallas_call | solution.py:811
  83.2 0.8 hand_on.1

commit v10 on v9

--- a/solution.py
+++ b/solution.py
@@ -201,6 +201,9 @@
         e = xor(mine8, 4 * far)
         return feed_copy(joint.at[f, part8(e), own_cols], f, e, feed_y.at[f, far], {"mp": across_y})
 
+    def hop(f):
+        return feed_copy(joint.at[f, part8(mine8), far_cols], f, mine8, feed_y.at[f, 1], {"graph": xor(g, 4)})
+
     def near(f, far, k):
         e = xor(mine8, 4 * far)
         return feed_copy(joint.at[f, part8(e), far_cols], f, e, near_recv.at[f, far, 0 if k == 2 - far else 1], {"graph": xor(g, k)})
@@ -396,8 +399,6 @@
     up_copy(0).start()
     if feeds:
         enter(0, 1).start()
-    for f in range(1, feeds):
-        enter(f, 0).start()
     step_rows = min(slot_total, 512)
     own = pl.ds(pl.multiple_of(g * cap, cap), cap)
     span = pl.ds(0, slot_total - cap)
@@ -467,7 +468,7 @@
             up_home()
         with scope("s_feedspread"):
             for f in range(1, feeds):
-                enter(f, 1).start()
+                enter(f, 0).start()
             if feeds:
                 for far in range(2):
                     enter(0, far).wait_recv()
@@ -569,6 +570,9 @@
             send(1, 0, c)
         if feeds:
             with scope("s_corner0"):
+                for f in range(1, feeds):
+                    enter(f, 0).wait_recv()
+                    hop(f).start()
                 for far in range(2):
                     feed_corner(0, far)
         sum1.drain()
@@ -614,10 +618,8 @@
     with scope("s_layer0"):
         with scope("s_feedrest0"):
             for f in range(1, feeds):
-                for far in range(2):
-                    enter(f, far).wait_recv()
-                    near(f, far, 2 - far).start()
-                    near(f, far, 1 + far).start()
+                near(f, 0, 2).start()
+                near(f, 0, 1).start()
         with scope("s_l0rel"):
             relay(1, 0, order[0])
         for spot, c in enumerate(order):
@@ -634,8 +636,11 @@
                 acts[1, m, chunk(c), :] = value
                 send(2, 1, c)
             with scope("s_l0feed%d" % spot):
-                if spot == 2:
+                if spot + 1 == len(order):
                     for f in range(1, feeds):
+                        hop(f).wait_recv()
+                        near(f, 1, 1).start()
+                        near(f, 1, 2).start()
                         feed_corner(f, 0)
 
     def layer_step(l, _):

time: 84.2 us -> 81.9 us (0.973)
  Pallas kernels: 83.3 us -> 80.9 us
    pallas_call x1, Pallas kernels: 82.5 us -> 80.2 us  [local(): pl.pallas_call(body, out_shape=(pltpu.VMEM((rows, width), bf16), pltpu.VM...]
where the time goes in v10:
time: 81.9 us; the launch traced here: 81.7 us
  Pallas kernels  80.9 us (99%)
    pallas_call x1, Pallas kernels, local(): pl.pallas_call(body, out_shape=(pltpu.VMEM((rows, width), bf16), pltpu.VM...  80.2 us

profile of v10, /device:TPU:0, one launch (start us, length us, event | category | flops | bytes accessed | tf_op | source)
XLA Modules:
  0.0 81.7 jit_solution(17525308372405635148)
XLA Ops:
  0.6 80.2 %edge_block.1 = (bf16[512,384]{1,0:T(8,128)(2,1)S(1)}, bf16[32,384]{1,0:T(8,128)(2,1)S(1)}) custom-call(bf16[512,384]{1,0:T(8,128)(2,1)} %state_hbm.1, bf16[384,384]{1,0:T(8,128)(2,1)} %down_hbm.1, f32[42,4096]{1,0:T(8,128)} %basis_hbm.1, f32[42,384]{1,0:T(8,128)} %bw_hbm.1, bf16[384,384]{1,0:T(8,128)(2,1)} %up_hbm.1, bf16[6,1536,384]{2,1,0:T(8,128)(2,1)} %bitcast.5, ...), custom_call_target="tpu_custom_call" | custom-call | tf_op jit(solution)/shard_map/edge_block/pallas_call | solution.py:816
  80.8 0.8 hand_on.1

commit v11 on v10

--- a/solution.py
+++ b/solution.py
@@ -573,8 +573,6 @@
                 for f in range(1, feeds):
                     enter(f, 0).wait_recv()
                     hop(f).start()
-                for far in range(2):
-                    feed_corner(0, far)
         sum1.drain()
         arrived(from_a.at[:, span], 0, 0).wait_send()
         arrived(from_b.at[:, span], 1, 0).wait_send()
@@ -616,12 +614,15 @@
         return value.astype(bf16)
 
     with scope("s_layer0"):
+        with scope("s_l0rel"):
+            relay(1, 0, order[0])
+        if feeds:
+            for far in range(2):
+                feed_corner(0, far)
         with scope("s_feedrest0"):
             for f in range(1, feeds):
                 near(f, 0, 2).start()
                 near(f, 0, 1).start()
-        with scope("s_l0rel"):
-            relay(1, 0, order[0])
         for spot, c in enumerate(order):
             with scope("s_l0fin%d" % spot):
                 finish(1, 0, c)

time: 81.9 us -> 81.9 us (level)
  no operation moved by 1% of the time
where the time goes in v11:
time: 81.9 us; the launch traced here: 81.7 us
  Pallas kernels  80.9 us (99%)
    pallas_call x1, Pallas kernels, local(): pl.pallas_call(body, out_shape=(pltpu.VMEM((rows, width), bf16), pltpu.VM...  80.2 us

profile of v11, /device:TPU:0, one launch (start us, length us, event | category | flops | bytes accessed | tf_op | source)
XLA Modules:
  0.0 81.7 jit_solution(13642844050694375477)
XLA Ops:
  0.6 80.2 %edge_block.1 = (bf16[512,384]{1,0:T(8,128)(2,1)S(1)}, bf16[32,384]{1,0:T(8,128)(2,1)S(1)}) custom-call(bf16[512,384]{1,0:T(8,128)(2,1)} %state_hbm.1, bf16[384,384]{1,0:T(8,128)(2,1)} %down_hbm.1, f32[42,4096]{1,0:T(8,128)} %basis_hbm.1, f32[42,384]{1,0:T(8,128)} %bw_hbm.1, bf16[384,384]{1,0:T(8,128)(2,1)} %up_hbm.1, bf16[6,1536,384]{2,1,0:T(8,128)(2,1)} %bitcast.5, ...), custom_call_target="tpu_custom_call" | custom-call | tf_op jit(solution)/shard_map/edge_block/pallas_call | solution.py:817
  80.8 0.8 hand_on.1
